TPU v7x, 512 devices: a whole 4x4x16 slice. The times are simulated.
512 devices in a mesh: gx: 4 (over y_hi, core), gy: 16 (over z), gz: 8 (over y_lo, x).
Axes of the slice: x: 4, y: 4 (y_hi: 2, y_lo: 2; y = y_hi * 2 + y_lo), z: 16, core: 2. Of those that a mesh axis runs over, the one named last changes fastest.
Arguments:
- heat_level_grid: float32 [256, 1024, 512], P('gz', 'gy', 'gx'), may hold values from -16 to 16, as said below
- interval_first_class: int32 [1], replicated, may hold values from 0 to 95
- interval_beyond_class: int32 [1], replicated, may hold values from 128 to 256
Outputs:
- magnitude: float32 [256, 1024, 512], P('gz', 'gy', 'gx')
- histogram: float32 [256], replicated
- stats: float32 [4], replicated
Inputs may be any that keep to these rules, and one draw needn't show every extreme that they name: `heat_level_grid`: each entry is a rough value times an amplitude that is constant on blocks of 8 x 4 x 4 cells (z, y, x) and varies over a factor of 16 between blocks.
All inputs are finite; a program needn't handle non-finite values.
Results may differ from a plain program's by a relative error of at most 0.0003.
Values sent between devices are 32-bit elements; how exact they have to be, the bound alone decides.
No kernel may reach another device: no remote copies, remote signals or barrier semaphores. Data moves between devices by JAX's collectives and lax.ppermute only.
A program may use at most 64 MiB of HBM per device.

v0:
```python
import jax
import jax.numpy as jnp
from jax import lax
from jax.sharding import Mesh
from jax.sharding import PartitionSpec as P

BINS = 256
GX = ("gx_0", "gx_1")
GZ = ("gz_0", "gz_1")
GX_GY_GZ = ("gx_0", "gx_1", "gy", "gz_0", "gz_1")


stencil_coefficients = (0.8, -0.2, 4.0 / 105.0, -1.0 / 280.0)
grad_range = 12.0


def extended_2(block, sides, width):
    for axis, dim in sides:
        count = lax.axis_size(axis)
        forward = [(i, i + 1) for i in range(count - 1)]
        forward.append((count - 1, 0))
        backward = [(target, source) for source, target in forward]
        low = lax.ppermute(
            lax.slice_in_dim(block, block.shape[dim] - width, None, axis=dim), axis, forward
        )
        high = lax.ppermute(lax.slice_in_dim(block, 0, width, axis=dim), axis, backward)
        block = jnp.concatenate([low, block, high], axis=dim)
    return block


def gathered_once(x, axis):
    leaves = jax.tree.leaves(x)
    turns = sorted(range(len(leaves)), key=lambda k: -leaves[k].size)
    width = (1, *leaves[turns[0]].shape)[-1]
    lines = [
        jnp.pad(leaves[k].reshape(-1), (0, -leaves[k].size % width)).reshape(-1, width)
        for k in turns
    ]
    both, at, found = (lax.all_gather(jnp.concatenate(lines), axis), 0, {})
    for k, line in zip(turns, lines):
        piece = both[:, at : at + len(line)].reshape(len(both), -1)
        found[k] = piece[:, : leaves[k].size].reshape(-1, *leaves[k].shape)
        at += len(line)
    numbers = iter(range(len(leaves)))
    return jax.tree.map(lambda _: found[next(numbers)], x)


def merged_by_axis(x, axes, combine):
    for axis in axes:
        pieces = gathered_once(x, axis)
        x = jax.tree.map(lambda part: part[0], pieces)
        for k in range(1, lax.axis_size(axis)):
            x = combine(x, jax.tree.map(lambda part: part[k], pieces))
    return x


def directional_rate(extended, direction_length_count):
    length = extended.shape[direction_length_count] - 8
    running = jnp.zeros(
        extended.shape[:direction_length_count]
        + (length,)
        + extended.shape[direction_length_count + 1 :],
        jnp.float32,
    )
    for offset, coefficient in enumerate(stencil_coefficients, start=1):
        forward_cells = lax.slice_in_dim(
            extended, 4 + offset, 4 + offset + length, axis=direction_length_count
        )
        backward_cells = lax.slice_in_dim(
            extended, 4 - offset, 4 - offset + length, axis=direction_length_count
        )
        running = running + coefficient * (forward_cells - backward_cells)
    return running


def local_counts(low_bin, fraction):
    cell_count = low_bin.shape[0]
    span_cells = min(cell_count, 32768)
    turn_count = cell_count // span_cells
    coarse_rows = BINS // 16
    coarse_ids = jnp.arange(coarse_rows, dtype=jnp.int32)[:, None]
    finer_ids = jnp.arange(16, dtype=jnp.int32)[:, None]

    def one_turn(turn_index, running):
        start = turn_index * span_cells
        low_part = lax.dynamic_slice_in_dim(low_bin, start, span_cells)
        frac_part = lax.dynamic_slice_in_dim(fraction, start, span_cells)
        high_part = low_part + 1
        coarse = jnp.concatenate([low_part // 16, high_part // 16])
        finer = jnp.concatenate([low_part % 16, high_part % 16])
        weight = jnp.concatenate([1.0 - frac_part, frac_part])
        left_side = jnp.where(coarse[None, :] == coarse_ids, weight[None, :], 0.0)
        right_side = (finer[None, :] == finer_ids).astype(jnp.float32)
        product = lax.dot_general(
            left_side,
            right_side,
            (((1,), (1,)), ((), ())),
            precision=lax.Precision.HIGHEST,
            preferred_element_type=jnp.float32,
        )
        return running + product

    running = lax.fori_loop(0, turn_count, one_turn, jnp.zeros((coarse_rows, 16), jnp.float32))
    return running.reshape(BINS)


def combine_all(first, second):
    return (
        first[0] + second[0],
        first[1] + second[1],
        first[2] + second[2],
        jnp.maximum(first[3], second[3]),
        jnp.minimum(first[4], second[4]),
    )


def on_device(heat_level_grid, interval_first_class, interval_beyond_class):
    grad_x = directional_rate(extended_2(heat_level_grid, ((GX, 2),), 4), 2)
    grad_y = directional_rate(extended_2(heat_level_grid, (("gy", 1),), 4), 1)
    grad_z = directional_rate(extended_2(heat_level_grid, ((GZ, 0),), 4), 0)
    slope_norm_square = grad_z * grad_z + grad_y * grad_y + grad_x * grad_x
    magnitude = jnp.sqrt(slope_norm_square + 1.0) - 1.0
    position = jnp.clip(magnitude * (BINS / grad_range), 0.5, BINS - 0.5)
    low_bin = jnp.minimum(jnp.floor(position - 0.5), BINS - 2).astype(jnp.int32)
    fraction = position - 0.5 - low_bin.astype(jnp.float32)
    counts = local_counts(low_bin.reshape(-1), fraction.reshape(-1))
    lower_edge = interval_first_class[0]
    upper_edge = interval_beyond_class[0]
    high_bin = low_bin + 1
    inside_low = (low_bin >= lower_edge) & (low_bin < upper_edge)
    inside_high = (high_bin >= lower_edge) & (high_bin < upper_edge)
    weight = jnp.where(inside_low, 1.0 - fraction, 0.0) + jnp.where(inside_high, fraction, 0.0)
    lowest = jnp.min(magnitude + grad_range * (1.0 - weight))
    highest = jnp.max(weight * magnitude)
    weighted_sum = jnp.sum(weight * magnitude)
    weighted_count = jnp.sum(weight)
    counts, weighted_sum, weighted_count, highest, lowest = merged_by_axis(
        (counts, weighted_sum, weighted_count, highest, lowest), GX_GY_GZ, combine_all
    )
    total_cells = (
        heat_level_grid.shape[0]
        * heat_level_grid.shape[1]
        * heat_level_grid.shape[2]
        * lax.axis_size(GX)
        * lax.axis_size("gy")
        * lax.axis_size(GZ)
    )
    histogram = counts * (BINS / total_cells)
    stats = jnp.stack([lowest, highest, weighted_sum / total_cells, weighted_count / total_cells])
    return (magnitude, histogram, stats)


def solution(mesh):
    finer = Mesh(
        mesh.devices.reshape(2, 2, mesh.shape["gy"], 2, 4), ("gx_0", "gx_1", "gy", "gz_0", "gz_1")
    )
    return jax.shard_map(
        on_device,
        mesh=finer,
        in_specs=(P(GZ, "gy", GX), P(), P()),
        out_specs=(P(GZ, "gy", GX), P(), P()),
        check_vma=False,
    )
```

profile of v0, /device:TPU:24, one launch (start us, length us, event | category | flops | bytes accessed | tf_op | source)
XLA Modules:
  0.0 224.6 jit_solution(5636302203498421307)
XLA Ops:
  0.6 1.6 fusion.69
  2.3 3.4 %collective-permute-start.1 = (f32[4,64,128]{2,1,0:T(8,128)}, f32[4,64,128]{2,1,0:T(8,128)S(1)}, u32[]{:S(2)}, u32[]{:S(2)}) collective-permute-start(f32[4,64,128]{2,1,0:T(8,128)} %get-tuple-element.248), channel_id=1, source_target_pairs={{0,1},{1,2},{2,3},{3,4},{4,5},{5,6},{6,7},{7,0},{8,9},{9,10},{10,1... | collective-permute-start | bytes 393224 | tf_op jit(solution)/shard_map/ppermute | solution.py:23
  5.7 4.6 %collective-permute-start = (f32[4,64,128]{2,1,0:T(8,128)S(1)}, f32[4,64,128]{2,1,0:T(8,128)S(1)}, u32[]{:S(2)}, u32[]{:S(2)}) collective-permute-start(f32[4,64,128]{2,1,0:T(8,128)S(1)} %get-tuple-element.247), channel_id=1, source_target_pairs={{1,0},{2,1},{3,2},{4,3},{5,4},{6,5},{7,6},{0,7},{9,8},{10,9},{11,1... | collective-permute-start | bytes 393224 | tf_op jit(solution)/shard_map/ppermute | solution.py:26
  10.2 1.9 fusion.71
  13.2 1.9 collective-permute-start.5
  15.5 5.1 %collective-permute-start.4 = (f32[32,64,4]{1,0,2:T(8,128)S(1)}, f32[32,64,4]{1,0,2:T(8,128)}, u32[]{:S(2)}, u32[]{:S(2)}) collective-permute-start(f32[32,64,4]{1,0,2:T(8,128)S(1)} %copy.31), channel_id=1, source_target_pairs={{128,0},{256,128},{384,256},{0,384},{129,1},{257,129},{385,257},{1... | collective-permute-start | bytes 98312 | tf_op jit(solution)/shard_map/ppermute | solution.py:26
  21.3 11.4 %collective-permute-start.2 = (f32[32,4,128]{2,1,0:T(4,128)}, f32[32,4,128]{2,1,0:T(4,128)}, u32[]{:S(2)}, u32[]{:S(2)}) collective-permute-start(f32[32,4,128]{2,1,0:T(4,128)} %get-tuple-element.252), channel_id=1, source_target_pairs={{8,0},{16,8},{24,16},{32,24},{40,32},{48,40},{56,48},{64,56},{72,6... | collective-permute-start | bytes 196616 | tf_op jit(solution)/shard_map/ppermute | solution.py:26
  34.0 1.9 collective-permute-start.3
  38.9 2.8 %collective-permute-done.3 = f32[32,4,128]{2,1,0:T(4,128)} collective-permute-done((f32[32,4,128]{2,1,0:T(4,128)}, f32[32,4,128]{2,1,0:T(4,128)}, u32[]{:S(2)}, u32[]{:S(2)}) %collective-permute-start.3) | collective-permute-done | bytes 65568 | tf_op jit(solution)/shard_map/ppermute | solution.py:23
  41.7 6.2 %add_reduce_fusion = (f32[]{:T(128)}, f32[]{:T(128)}, f32[]{:T(128)}, f32[]{:T(128)}, f32[32,64,128]{2,1,0:T(8,128)S(1)}) fusion(s32[]{:T(128)} %bitcast.122, s32[]{:T(128)} %bitcast.121, f32[32,64,128]{2,1,0:T(8,128)S(1)} %copy-done, f32[32,64,4]{2,1,0:T(8,128)S(1)} %copy.10, f32[32,64,4]{2,1,0:T(8,128)S(1)} %copy.8, ...), kind=kLoop, calls=%fused_computation.103 | loop fusion | flops 20709376 | bytes 14811160 | tf_op jit(solution)/shard_map/reduce_min | solution.py:133
  49.3 43.6 %while.18 = (s32[]{:T(128)}, f32[16,16]{1,0:T(8,128)S(1)}, s32[262144]{0:T(1024)S(1)}, f32[262144]{0:T(1024)}, s32[]{:T(128)}, /*index=5*/s32[]{:T(128)}, s32[]{:T(128)}, s32[]{:T(128)}) while((s32[]{:T(128)}, f32[16,16]{1,0:T(8,128)S(1)}, s32[262144]{0:T(1024)S(1)}, f32[262144]{0:T(1024)}, s32[]{:T(128)}, ...), condition=%wide.region_1.2_spmd.clone.clone, body=%wide.region_0.1_spmd.clone.clone.sunk | while | flops 206176768 | bytes 5703833 | solution.py:103
  51.2 3.6 %fusion.106 = f32[16,16]{1,0:T(8,128)S(1)} fusion(f32[65536]{0:T(1024)S(1)} %pad_maximum_fusion.6, s32[65536]{0:T(1024)S(1)} %get-tuple-element.425, f32[16,16]{1,0:T(8,128)S(1)} %get-tuple-element.436, pred[]{:T(512)S(6)} %compare.49, pred[16,65536]{1,0:T(8,128)(4,1)S(1)} %iota_compare_fusion.11), kind=kOutput, calls=%fused_computation.9.clone.3 | convolution fusion | flops 203424256 | bytes 1574913 | tf_op jit(solution)/shard_map/while/body/eval_jaxpr/dot_general | solution.py:94
  56.6 3.6 %fusion.106 = f32[16,16]{1,0:T(8,128)S(1)} fusion(f32[65536]{0:T(1024)S(1)} %pad_maximum_fusion.6, s32[65536]{0:T(1024)S(1)} %get-tuple-element.425, f32[16,16]{1,0:T(8,128)S(1)} %get-tuple-element.436, pred[]{:T(512)S(6)} %compare.49, pred[16,65536]{1,0:T(8,128)(4,1)S(1)} %iota_compare_fusion.11), kind=kOutput, calls=%fused_computation.9.clone.3 | convolution fusion | flops 203424256 | bytes 1574913 | tf_op jit(solution)/shard_map/while/body/eval_jaxpr/dot_general | solution.py:94
  62.1 3.6 %fusion.106 = f32[16,16]{1,0:T(8,128)S(1)} fusion(f32[65536]{0:T(1024)S(1)} %pad_maximum_fusion.6, s32[65536]{0:T(1024)S(1)} %get-tuple-element.425, f32[16,16]{1,0:T(8,128)S(1)} %get-tuple-element.436, pred[]{:T(512)S(6)} %compare.49, pred[16,65536]{1,0:T(8,128)(4,1)S(1)} %iota_compare_fusion.11), kind=kOutput, calls=%fused_computation.9.clone.3 | convolution fusion | flops 203424256 | bytes 1574913 | tf_op jit(solution)/shard_map/while/body/eval_jaxpr/dot_general | solution.py:94
  67.5 3.6 %fusion.106 = f32[16,16]{1,0:T(8,128)S(1)} fusion(f32[65536]{0:T(1024)S(1)} %pad_maximum_fusion.6, s32[65536]{0:T(1024)S(1)} %get-tuple-element.425, f32[16,16]{1,0:T(8,128)S(1)} %get-tuple-element.436, pred[]{:T(512)S(6)} %compare.49, pred[16,65536]{1,0:T(8,128)(4,1)S(1)} %iota_compare_fusion.11), kind=kOutput, calls=%fused_computation.9.clone.3 | convolution fusion | flops 203424256 | bytes 1574913 | tf_op jit(solution)/shard_map/while/body/eval_jaxpr/dot_general | solution.py:94
  73.0 3.6 %fusion.106 = f32[16,16]{1,0:T(8,128)S(1)} fusion(f32[65536]{0:T(1024)S(1)} %pad_maximum_fusion.6, s32[65536]{0:T(1024)S(1)} %get-tuple-element.425, f32[16,16]{1,0:T(8,128)S(1)} %get-tuple-element.436, pred[]{:T(512)S(6)} %compare.49, pred[16,65536]{1,0:T(8,128)(4,1)S(1)} %iota_compare_fusion.11), kind=kOutput, calls=%fused_computation.9.clone.3 | convolution fusion | flops 203424256 | bytes 1574913 | tf_op jit(solution)/shard_map/while/body/eval_jaxpr/dot_general | solution.py:94
  78.4 3.6 %fusion.106 = f32[16,16]{1,0:T(8,128)S(1)} fusion(f32[65536]{0:T(1024)S(1)} %pad_maximum_fusion.6, s32[65536]{0:T(1024)S(1)} %get-tuple-element.425, f32[16,16]{1,0:T(8,128)S(1)} %get-tuple-element.436, pred[]{:T(512)S(6)} %compare.49, pred[16,65536]{1,0:T(8,128)(4,1)S(1)} %iota_compare_fusion.11), kind=kOutput, calls=%fused_computation.9.clone.3 | convolution fusion | flops 203424256 | bytes 1574913 | tf_op jit(solution)/shard_map/while/body/eval_jaxpr/dot_general | solution.py:94
  83.9 3.6 %fusion.106 = f32[16,16]{1,0:T(8,128)S(1)} fusion(f32[65536]{0:T(1024)S(1)} %pad_maximum_fusion.6, s32[65536]{0:T(1024)S(1)} %get-tuple-element.425, f32[16,16]{1,0:T(8,128)S(1)} %get-tuple-element.436, pred[]{:T(512)S(6)} %compare.49, pred[16,65536]{1,0:T(8,128)(4,1)S(1)} %iota_compare_fusion.11), kind=kOutput, calls=%fused_computation.9.clone.3 | convolution fusion | flops 203424256 | bytes 1574913 | tf_op jit(solution)/shard_map/while/body/eval_jaxpr/dot_general | solution.py:94
  89.3 3.6 %fusion.106 = f32[16,16]{1,0:T(8,128)S(1)} fusion(f32[65536]{0:T(1024)S(1)} %pad_maximum_fusion.6, s32[65536]{0:T(1024)S(1)} %get-tuple-element.425, f32[16,16]{1,0:T(8,128)S(1)} %get-tuple-element.436, pred[]{:T(512)S(6)} %compare.49, pred[16,65536]{1,0:T(8,128)(4,1)S(1)} %iota_compare_fusion.11), kind=kOutput, calls=%fused_computation.9.clone.3 | convolution fusion | flops 203424256 | bytes 1574913 | tf_op jit(solution)/shard_map/while/body/eval_jaxpr/dot_general | solution.py:94
  95.5 5.9 %all-gather.5 = f32[2,5,256]{2,1,0:T(8,128)S(1)} all-gather(f32[1,5,256]{2,1,0:T(8,128)S(1)} %bitcast.128), channel_id=2, replica_groups=mesh['gx_0'=2,'gx_1'=2,'gy'=16,'gz_0'=2,'gz_1'=4] {'gx_0'}, dimensions={0}, use_global_device_ids=true | all-gather | bytes 15360 | tf_op jit(solution)/shard_map/all_gather | solution.py:39
  108.8 1.8 all-gather.6
  118.0 27.0 %all-gather.7 = f32[16,5,256]{2,1,0:T(8,128)S(1)} all-gather(f32[1,5,256]{2,1,0:T(8,128)S(1)} %bitcast.130), channel_id=4, replica_groups=mesh['gx_0'=2,'gx_1'=2,'gy'=16,'gz_0'=2,'gz_1'=4] {'gy'}, dimensions={0}, use_global_device_ids=true | all-gather | bytes 87040 | tf_op jit(solution)/shard_map/all_gather | solution.py:39
  187.5 4.4 %all-gather.8 = f32[2,5,256]{2,1,0:T(8,128)S(1)} all-gather(f32[1,5,256]{2,1,0:T(8,128)S(1)} %bitcast.131), channel_id=5, replica_groups=mesh['gx_0'=2,'gx_1'=2,'gy'=16,'gz_0'=2,'gz_1'=4] {'gz_0'}, dimensions={0}, use_global_device_ids=true | all-gather | bytes 15360 | tf_op jit(solution)/shard_map/all_gather | solution.py:39
  199.3 11.9 %all-gather.9 = f32[4,5,256]{2,1,0:T(8,128)S(1)} all-gather(f32[1,5,256]{2,1,0:T(8,128)S(1)} %bitcast.132), channel_id=6, replica_groups=mesh['gx_0'=2,'gx_1'=2,'gy'=16,'gz_0'=2,'gz_1'=4] {'gz_1'}, dimensions={0}, use_global_device_ids=true | all-gather | bytes 25600 | tf_op jit(solution)/shard_map/all_gather | solution.py:39
  (143 shorter events, 36.1 us)
Async XLA Ops:
  2.3 35.3 %collective-permute-start.1 = (f32[4,64,128]{2,1,0:T(8,128)}, f32[4,64,128]{2,1,0:T(8,128)S(1)}, u32[]{:S(2)}, u32[]{:S(2)}) collective-permute-start(f32[4,64,128]{2,1,0:T(8,128)} %get-tuple-element.248), channel_id=1, source_target_pairs={{0,1},{1,2},{2,3},{3,4},{4,5},{5,6},{6,7},{7,0},{8,9},{9,10},{10,1... | collective-permute-start | bytes 393224 | tf_op jit(solution)/shard_map/ppermute | solution.py:23
  5.7 32.3 %collective-permute-start = (f32[4,64,128]{2,1,0:T(8,128)S(1)}, f32[4,64,128]{2,1,0:T(8,128)S(1)}, u32[]{:S(2)}, u32[]{:S(2)}) collective-permute-start(f32[4,64,128]{2,1,0:T(8,128)S(1)} %get-tuple-element.247), channel_id=1, source_target_pairs={{1,0},{2,1},{3,2},{4,3},{5,4},{6,5},{7,6},{0,7},{9,8},{10,9},{11,1... | collective-permute-start | bytes 393224 | tf_op jit(solution)/shard_map/ppermute | solution.py:26
  12.2 8.5 %copy-start = (f32[32,64,128]{2,1,0:T(8,128)S(1)}, f32[32,64,128]{2,1,0:T(8,128)}, u32[]{:S(2)}) copy-start(f32[32,64,128]{2,1,0:T(8,128)} %param.5) | copy-start | bytes 3145732
  13.2 20.8 %collective-permute-start.5 = (f32[32,64,4]{1,0,2:T(8,128)}, f32[32,64,4]{1,0,2:T(8,128)S(1)}, u32[]{:S(2)}, u32[]{:S(2)}) collective-permute-start(f32[32,64,4]{1,0,2:T(8,128)} %copy.32), channel_id=1, source_target_pairs={{0,128},{128,256},{256,384},{384,0},{1,129},{129,257},{257,385},{3... | collective-permute-start | bytes 98312 | tf_op jit(solution)/shard_map/ppermute | solution.py:23
  15.5 20.9 %collective-permute-start.4 = (f32[32,64,4]{1,0,2:T(8,128)S(1)}, f32[32,64,4]{1,0,2:T(8,128)}, u32[]{:S(2)}, u32[]{:S(2)}) collective-permute-start(f32[32,64,4]{1,0,2:T(8,128)S(1)} %copy.31), channel_id=1, source_target_pairs={{128,0},{256,128},{384,256},{0,384},{129,1},{257,129},{385,257},{1... | collective-permute-start | bytes 98312 | tf_op jit(solution)/shard_map/ppermute | solution.py:26
  21.3 16.7 %collective-permute-start.2 = (f32[32,4,128]{2,1,0:T(4,128)}, f32[32,4,128]{2,1,0:T(4,128)}, u32[]{:S(2)}, u32[]{:S(2)}) collective-permute-start(f32[32,4,128]{2,1,0:T(4,128)} %get-tuple-element.252), channel_id=1, source_target_pairs={{8,0},{16,8},{24,16},{32,24},{40,32},{48,40},{56,48},{64,56},{72,6... | collective-permute-start | bytes 196616 | tf_op jit(solution)/shard_map/ppermute | solution.py:26
  34.0 7.7 %collective-permute-start.3 = (f32[32,4,128]{2,1,0:T(4,128)}, f32[32,4,128]{2,1,0:T(4,128)}, u32[]{:S(2)}, u32[]{:S(2)}) collective-permute-start(f32[32,4,128]{2,1,0:T(4,128)} %get-tuple-element.253), channel_id=1, source_target_pairs={{0,8},{8,16},{16,24},{24,32},{32,40},{40,48},{48,56},{56,64},{64,7... | collective-permute-start | bytes 196616 | tf_op jit(solution)/shard_map/ppermute | solution.py:23
  47.9 1.4 copy-start.1
where the time goes:
time: 226 us; the launch traced here: 225 us
  between operations  67.5 us (30%)
  blocking collectives  51 us (23%)
  matrix products  28.5 us (13%)
  starting transfers between devices  28.3 us (13%)
  other arithmetic  23.3 us (10%)
  local copies, waits for them, and re-layouts  22.6 us (10%)
  waiting for transfers between devices  2.81 us (1%)
    all_gather x5, blocking collectives, gathered_once(): both, at, found = (lax.all_gather(jnp.concatenate(lines), axis), 0, {})  51 us
    dot_general x8, matrix products, one_turn(): lax.dot_general(left_side, right_side, (((1,), (1,)), ((), ())), precisio...  28.5 us
    ppermute x3, starting transfers between devices, extended_2(): lax.ppermute(lax.slice_in_dim(block, 0, width, axis=dim), axis, backward)  21.1 us
    slice x20, local copies, waits for them, and re-layouts, merged_by_axis(): x = combine(x, jax.tree.map(lambda part: part[k], pieces))  11.2 us
    sub x8, other arithmetic, one_turn(): weight = jnp.concatenate([1.0 - frac_part, frac_part])  7.43 us
    ppermute x3, starting transfers between devices, extended_2(): lax.ppermute(lax.slice_in_dim(block, block.shape[dim] - width, None, axis...  7.22 us
    reduce_min x1, other arithmetic, on_device(): lowest = jnp.min(magnitude + grad_range * (1.0 - weight))  6.22 us
  transfers between devices with their start and end apart: 6, of which 1 were waited for; matrix products, arithmetic and copies ran while one was open for 3% of the time, Pallas kernels for 0%

commit v1 on v0

v1 whole, which is shorter than its diff:
```python
import jax
import jax.numpy as jnp
import numpy as np
from jax import lax
from jax.experimental import pallas as pl
from jax.experimental.pallas import tpu as pltpu
from jax.sharding import Mesh
from jax.sharding import PartitionSpec as P

BINS = 256
GX = ("gx_0", "gx_1")
GZ = ("gz_0", "gz_1")
GX_GZ = ("gx_0", "gx_1", "gz_0", "gz_1")
COEF = tuple(float(np.float32(c)) for c in (0.8, -0.2, 4.0 / 105.0, -1.0 / 280.0))
GRAD_RANGE = 12.0
NZ, NY, NX = 32, 64, 128
STRIDE = NY + 16
ROUNDER = 49152.0


def split3(a):
    high = a.astype(jnp.bfloat16)
    rest = a - high.astype(jnp.float32)
    mid = rest.astype(jnp.bfloat16)
    low = (rest - mid.astype(jnp.float32)).astype(jnp.bfloat16)
    return high, mid, low


def correction_matrix():
    table = np.zeros((8, NX), np.float32)
    for j in range(4):
        for k in range(1, 5):
            i = NX + j - k
            if i < NX:
                table[j, i] = COEF[k - 1]
            i = k - 4 + j
            if i >= 0:
                table[4 + j, i] = -COEF[k - 1]
    high = table.astype(jnp.bfloat16)
    rest = table - high.astype(np.float32)
    mid = rest.astype(jnp.bfloat16)
    low = (rest - mid.astype(np.float32)).astype(jnp.bfloat16)
    return np.concatenate([high, mid, high, low, mid, high], axis=0)


def pack_kernel(x_ref, xlo_ref, xhi_ref, ylo_ref, yhi_ref, zlo_ref, zhi_ref):
    for i in range(NZ * NY // 128):
        block = x_ref[2 * i : 2 * i + 2].reshape(128, NX)
        turned = block.T
        xlo_ref[:, i * 128 : (i + 1) * 128] = turned[0:4]
        xhi_ref[:, i * 128 : (i + 1) * 128] = turned[NX - 4 :]
    ylo_ref[...] = x_ref[:, 0:4, :]
    yhi_ref[...] = x_ref[:, NY - 4 :, :]
    zlo_ref[...] = x_ref[0:4]
    zhi_ref[...] = x_ref[NZ - 4 :]


def pack(x):
    f32 = jnp.float32
    return pl.pallas_call(
        pack_kernel,
        out_shape=(
            jax.ShapeDtypeStruct((4, NZ * NY), f32),
            jax.ShapeDtypeStruct((4, NZ * NY), f32),
            jax.ShapeDtypeStruct((NZ, 4, NX), f32),
            jax.ShapeDtypeStruct((NZ, 4, NX), f32),
            jax.ShapeDtypeStruct((4, NY, NX), f32),
            jax.ShapeDtypeStruct((4, NY, NX), f32),
        ),
        name="pack",
    )(x)


def main_kernel(
    first_ref, beyond_ref, c_ref, xlo_ref, xhi_ref, xleft_ref, xright_ref,
    x_hbm, ybelow_hbm, yabove_hbm, zbelow_hbm, zabove_hbm,
    mag_ref, red_ref,
    ext_ref, corr_ref, cell_ref, acc_ref, stat_ref, sems,
):
    copies = [
        pltpu.make_async_copy(x_hbm, ext_ref.at[4 : 4 + NZ, 8 : 8 + NY], sems.at[0]),
        pltpu.make_async_copy(zbelow_hbm, ext_ref.at[0:4, 8 : 8 + NY], sems.at[1]),
        pltpu.make_async_copy(zabove_hbm, ext_ref.at[4 + NZ :, 8 : 8 + NY], sems.at[2]),
        pltpu.make_async_copy(ybelow_hbm, ext_ref.at[4 : 4 + NZ, 4:8], sems.at[3]),
        pltpu.make_async_copy(yabove_hbm, ext_ref.at[4 : 4 + NZ, 8 + NY : 12 + NY], sems.at[4]),
    ]
    for copy in copies:
        copy.start()

    for i in range(NZ * NY // 128):
        cut = slice(i * 128, (i + 1) * 128)
        delta = jnp.concatenate(
            [xright_ref[:, cut] - xlo_ref[:, cut], xleft_ref[:, cut] - xhi_ref[:, cut]], axis=0
        )
        h, m, l = split3(delta)
        left = jnp.concatenate([h, h, m, h, m, l], axis=0)
        corr_ref[cut, :] = lax.dot_general(
            left, c_ref[...], (((0,), (0,)), ((), ())), preferred_element_type=jnp.float32
        )
    acc_ref[...] = jnp.zeros_like(acc_ref)
    stat_ref[0] = jnp.zeros((8, NX), jnp.float32)
    stat_ref[1] = jnp.full((8, NX), -3.0e38, jnp.float32)
    stat_ref[2] = jnp.full((8, NX), 3.0e38, jnp.float32)
    for copy in copies:
        copy.wait()

    first = first_ref[0].astype(jnp.float32)
    beyond = beyond_ref[0].astype(jnp.float32)
    rows_ref = ext_ref.reshape((NZ + 8) * STRIDE, NX)
    ids = lax.broadcasted_iota(jnp.int32, (16, NX), 0).astype(jnp.float32).astype(jnp.bfloat16)

    def cells(z, slot):
        base = (z + 4) * STRIDE + 8

        def at(offset):
            return rows_ref[pl.ds(base + offset, NY), :]

        center = at(0)
        gz = gy = gx = None
        for k in range(1, 5):
            c = COEF[k - 1]
            dz = c * (at(k * STRIDE) - at(-k * STRIDE))
            dy = c * (at(k) - at(-k))
            dx = c * (pltpu.roll(center, NX - k, 1) - pltpu.roll(center, k, 1))
            gz = dz if gz is None else gz + dz
            gy = dy if gy is None else gy + dy
            gx = dx if gx is None else gx + dx
        gx = gx + corr_ref[pl.ds(pl.multiple_of(z * NY, NY), NY), :]
        norm = gz * gz + gy * gy + gx * gx
        mag = jnp.sqrt(norm + 1.0) - 1.0
        mag_ref[z] = mag
        place = jnp.clip(mag * (BINS / GRAD_RANGE), 0.5, BINS - 0.5) - 0.5
        low = jnp.minimum(jnp.floor(place), BINS - 2.0)
        frac = place - low
        inside_low = (low >= first) & (low < beyond)
        inside_high = (low >= first - 1.0) & (low < beyond - 1.0)
        weight = jnp.where(inside_low, 1.0 - frac, 0.0) + jnp.where(inside_high, frac, 0.0)
        wm = weight * mag
        bottom = mag + GRAD_RANGE * (1.0 - weight)
        parts = lambda a: a.reshape(NY // 8, 8, NX)
        stat_ref[0] += jnp.sum(parts(wm), axis=0)
        stat_ref[1] = jnp.maximum(stat_ref[1], jnp.max(parts(wm), axis=0))
        stat_ref[2] = jnp.minimum(stat_ref[2], jnp.min(parts(bottom), axis=0))
        coarse = jnp.floor(low * 0.0625)
        frac_high = (frac + ROUNDER) - ROUNDER
        cell_ref[slot, 0] = coarse
        cell_ref[slot, 1] = low - 16.0 * coarse
        cell_ref[slot, 2] = frac_high
        cell_ref[slot, 3] = frac - frac_high

    def hist(slot):
        one = jnp.ones((16, NX), jnp.bfloat16)
        zero = jnp.zeros((16, NX), jnp.bfloat16)
        ones, highs, lows, fines = [], [], [], []
        for g in range(8):
            og, hg, lg, fg = [], [], [], []
            for j in range(8):
                r = g * 8 + j

                def row(q):
                    return jnp.broadcast_to(cell_ref[slot, q, r : r + 1, :], (16, NX)).astype(jnp.bfloat16)

                mask = row(0) == ids
                og.append(jnp.where(mask, one, zero))
                hg.append(jnp.where(mask, row(2), zero))
                lg.append(jnp.where(mask, row(3), zero))
                fg.append(jnp.where(row(1) == ids, one, zero))
            ones.append(jnp.concatenate(og, axis=1))
            highs.append(jnp.concatenate(hg, axis=1))
            lows.append(jnp.concatenate(lg, axis=1))
            fines.append(jnp.concatenate(fg, axis=1))
        left = jnp.concatenate(ones + highs + lows, axis=0)
        right = jnp.concatenate(fines, axis=0)
        acc_ref[...] += lax.dot_general(
            left, right, (((1,), (1,)), ((), ())), preferred_element_type=jnp.float32
        )

    cells(0, 0)

    def step(z, carry):
        hist((z - 1) % 2)
        cells(z, z % 2)
        return carry

    lax.fori_loop(1, NZ, step, 0)
    hist((NZ - 1) % 2)

    lane = lax.broadcasted_iota(jnp.int32, (16, NX), 1)
    sub = lax.broadcasted_iota(jnp.int32, (16, NX), 0)
    sums = []
    for w in range(3):
        total = jnp.zeros((16, NX), jnp.float32)
        for g in range(8):
            at_row = w * 128 + g * 16
            total = total + jnp.where(lane // 16 == g, acc_ref[at_row : at_row + 16, :], 0.0)
        for shift in (64, 32, 16):
            total = total + pltpu.roll(total, shift, 1)
        sums.append(total)
    upper = sums[1] + sums[2]
    beside = pltpu.roll(upper, 1, 1)
    carried = jnp.where(sub == 0, 0.0, pltpu.roll(beside, 1, 0))
    counts = sums[0] - upper + jnp.where(lane % 16 == 0, carried, beside)
    tops = [
        jnp.sum(jnp.where(sub == 8 * h + lane // 16, counts, 0.0), axis=0, keepdims=True)
        for h in range(2)
    ]
    tile = jnp.concatenate(
        tops
        + [
            jnp.sum(stat_ref[0], axis=0, keepdims=True),
            jnp.max(stat_ref[1], axis=0, keepdims=True),
            jnp.min(stat_ref[2], axis=0, keepdims=True),
            jnp.zeros((3, NX), jnp.float32),
        ],
        axis=0,
    )
    red_ref[...] = jnp.broadcast_to(tile[None], red_ref.shape)


def main(x, edges, halos, first, beyond, peers):
    xlo, xhi = edges
    xleft, xright, ybelow, yabove, zbelow, zabove = halos
    smem = pl.BlockSpec(memory_space=pltpu.SMEM)
    vmem = pl.BlockSpec(memory_space=pltpu.VMEM)
    anywhere = pl.BlockSpec(memory_space=pl.ANY)
    return pl.pallas_call(
        main_kernel,
        in_specs=[smem, smem] + [vmem] * 5 + [anywhere] * 5,
        out_specs=(vmem, vmem),
        out_shape=(
            jax.ShapeDtypeStruct((NZ, NY, NX), jnp.float32),
            jax.ShapeDtypeStruct((peers, 8, NX), jnp.float32),
        ),
        scratch_shapes=[
            pltpu.VMEM((NZ + 8, STRIDE, NX), jnp.float32),
            pltpu.VMEM((NZ * NY, NX), jnp.float32),
            pltpu.VMEM((2, 4, NY, NX), jnp.float32),
            pltpu.VMEM((384, NX), jnp.float32),
            pltpu.VMEM((3, 8, NX), jnp.float32),
            pltpu.SemaphoreType.DMA((5,)),
        ],
        name="cells",
    )(first, beyond, correction_matrix(), xlo, xhi, xleft, xright, x, ybelow, yabove, zbelow, zabove)


def merged(a):
    summed = jnp.sum(a[:, 0:3, :], axis=0)
    high = jnp.max(a[:, 3:4, :], axis=0)
    low = jnp.min(a[:, 4:5, :], axis=0)
    return summed, high, low


def merge_kernel(a_ref, out_ref):
    summed, high, low = merged(a_ref)
    tile = jnp.concatenate([summed, high, low, jnp.zeros((3, NX), jnp.float32)], axis=0)
    out_ref[...] = jnp.broadcast_to(tile[None], out_ref.shape)


def final_kernel(first_ref, beyond_ref, a_ref, hist_ref, stats_ref):
    summed, high, low = merged(a_ref)
    cells = 134217728.0
    counts = summed[0:2]
    hist_ref[...] = counts * (BINS / cells)
    bins = lax.broadcasted_iota(jnp.int32, (2, NX), 0) * NX + lax.broadcasted_iota(jnp.int32, (2, NX), 1)
    inside = (bins >= first_ref[0]) & (bins < beyond_ref[0])
    stats_ref[0] = jnp.min(low)
    stats_ref[1] = jnp.max(high)
    stats_ref[2] = jnp.sum(summed[2:3]) / cells
    stats_ref[3] = jnp.sum(jnp.where(inside, counts, 0.0)) / cells


def shifted(part, axis, step):
    count = lax.axis_size(axis)
    return lax.ppermute(part, axis, [(i, (i + step) % count) for i in range(count)])


def on_device(x, first, beyond):
    xlo, xhi, ylo, yhi, zlo, zhi = pack(x)
    halos = (
        shifted(xhi, GX, 1),
        shifted(xlo, GX, -1),
        shifted(yhi, "gy", 1),
        shifted(ylo, "gy", -1),
        shifted(zhi, GZ, 1),
        shifted(zlo, GZ, -1),
    )
    mag, red = main(x, (xlo, xhi), halos, first, beyond, lax.axis_size(GX_GZ))
    red = lax.all_to_all(red, GX_GZ, 0, 0)
    red = pl.pallas_call(
        merge_kernel,
        out_shape=jax.ShapeDtypeStruct((lax.axis_size("gy"), 8, NX), jnp.float32),
        name="merge",
    )(red)
    red = lax.all_to_all(red, "gy", 0, 0)
    smem = pl.BlockSpec(memory_space=pltpu.SMEM)
    vmem = pl.BlockSpec(memory_space=pltpu.VMEM)
    hist, stats = pl.pallas_call(
        final_kernel,
        in_specs=[smem, smem, vmem],
        out_specs=(vmem, smem),
        out_shape=(
            jax.ShapeDtypeStruct((2, NX), jnp.float32),
            jax.ShapeDtypeStruct((4,), jnp.float32),
        ),
        name="final",
    )(first, beyond, red)
    return mag, hist.reshape(BINS), stats


def solution(mesh):
    finer = Mesh(
        mesh.devices.reshape(2, 2, mesh.shape["gy"], 2, 4), ("gx_0", "gx_1", "gy", "gz_0", "gz_1")
    )
    return jax.shard_map(
        on_device,
        mesh=finer,
        in_specs=(P(GZ, "gy", GX), P(), P()),
        out_specs=(P(GZ, "gy", GX), P(), P()),
        check_vma=False,
    )
```

time: 226 us -> 89.9 us (0.40)
  the two profiles are of different devices: /device:TPU:24 before, /device:TPU:1 now
where the time goes in v1:
time: 89.9 us; the launch traced here: 89.3 us
  blocking collectives  35.2 us (39%)
  starting transfers between devices  29.4 us (33%)
  Pallas kernels  21.4 us (24%)
  between operations  2.06 us (2%)
  local copies, waits for them, and re-layouts  1.29 us (1%)
    ppermute x6, starting transfers between devices, shifted(): lax.ppermute(part, axis, [(i, (i + step) % count) for i in range(count)])  29.4 us
    all_to_all x1, blocking collectives, on_device(): red = lax.all_to_all(red, 'gy', 0, 0)  20.3 us
    pallas_call x1, Pallas kernels, main(): pl.pallas_call(main_kernel, in_specs=[smem, smem] + [vmem] * 5 + [anywher...  16.1 us
    all_to_all x1, blocking collectives, on_device(): red = lax.all_to_all(red, GX_GZ, 0, 0)  14.9 us
    pallas_call x1, Pallas kernels, pack(): pl.pallas_call(pack_kernel, out_shape=(jax.ShapeDtypeStruct((4, NZ * NY),...  2.25 us
  transfers between devices with their start and end apart: 6, of which 0 were waited for; matrix products, arithmetic and copies ran while one was open for 0% of the time, Pallas kernels for 0%

profile of v1, /device:TPU:1, one launch (start us, length us, event | category | flops | bytes accessed | tf_op | source)
XLA Modules:
  0.0 89.3 jit_solution(9952644435799459049)
XLA Ops:
  0.6 2.3 %pack.1 = (f32[4,2048]{1,0:T(4,128)}, f32[4,2048]{1,0:T(4,128)}, f32[32,4,128]{2,1,0:T(4,128)}, f32[32,4,128]{2,1,0:T(4,128)}, f32[4,64,128]{2,1,0:T(8,128)}, /*index=5*/f32[4,64,128]{2,1,0:T(8,128)}) custom-call(f32[32,64,128]{2,1,0:T(8,128)} %x_hbm.1), custom_call_target="tpu_custom_call" | custom-call | tf_op jit(solution)/shard_map/pack/pallas_call | solution.py:60
  2.9 3.9 %collective-permute-start.4 = (f32[4,64,128]{2,1,0:T(8,128)}, f32[4,64,128]{2,1,0:T(8,128)S(1)}, u32[]{:S(2)}, u32[]{:S(2)}) collective-permute-start(f32[4,64,128]{2,1,0:T(8,128)} %get-tuple-element.17), channel_id=1, source_target_pairs={{0,1},{1,2},{2,3},{3,4},{4,5},{5,6},{6,7},{7,0},{8,9},{9,10},{10,1... | collective-permute-start | bytes 393224 | tf_op jit(solution)/shard_map/ppermute | solution.py:274
  6.8 4.2 %collective-permute-start.5 = (f32[4,64,128]{2,1,0:T(8,128)}, f32[4,64,128]{2,1,0:T(8,128)S(1)}, u32[]{:S(2)}, u32[]{:S(2)}) collective-permute-start(f32[4,64,128]{2,1,0:T(8,128)} %get-tuple-element.18), channel_id=1, source_target_pairs={{0,7},{1,0},{2,1},{3,2},{4,3},{5,4},{6,5},{7,6},{8,15},{9,8},{10,9... | collective-permute-start | bytes 393224 | tf_op jit(solution)/shard_map/ppermute | solution.py:274
  11.0 8.6 %collective-permute-start.1 = (f32[4,2048]{1,0:T(4,128)}, f32[4,2048]{1,0:T(4,128)S(1)}, u32[]{:S(2)}, u32[]{:S(2)}) collective-permute-start(f32[4,2048]{1,0:T(4,128)} %get-tuple-element.13.xlo_ref), channel_id=1, source_target_pairs={{0,384},{128,0},{256,128},{384,256},{1,385},{129,1},{257,129},{385... | collective-permute-start | bytes 98312 | tf_op jit(solution)/shard_map/ppermute | solution.py:274
  19.6 1.9 %collective-permute-start.2 = (f32[32,4,128]{2,1,0:T(4,128)}, f32[32,4,128]{2,1,0:T(4,128)S(1)}, u32[]{:S(2)}, u32[]{:S(2)}) collective-permute-start(f32[32,4,128]{2,1,0:T(4,128)} %get-tuple-element.15), channel_id=1, source_target_pairs={{0,8},{8,16},{16,24},{24,32},{32,40},{40,48},{48,56},{56,64},{64,7... | collective-permute-start | bytes 196616 | tf_op jit(solution)/shard_map/ppermute | solution.py:274
  21.5 5.8 %collective-permute-start.3 = (f32[32,4,128]{2,1,0:T(4,128)}, f32[32,4,128]{2,1,0:T(4,128)S(1)}, u32[]{:S(2)}, u32[]{:S(2)}) collective-permute-start(f32[32,4,128]{2,1,0:T(4,128)} %get-tuple-element.16), channel_id=1, source_target_pairs={{0,120},{8,0},{16,8},{24,16},{32,24},{40,32},{48,40},{56,48},{64,5... | collective-permute-start | bytes 196616 | tf_op jit(solution)/shard_map/ppermute | solution.py:274
  27.3 0.0 collective-permute-done.1.xright_ref
  27.3 5.0 %collective-permute-start = (f32[4,2048]{1,0:T(4,128)}, f32[4,2048]{1,0:T(4,128)S(1)}, u32[]{:S(2)}, u32[]{:S(2)}) collective-permute-start(f32[4,2048]{1,0:T(4,128)} %get-tuple-element.14.xhi_ref), channel_id=1, source_target_pairs={{0,128},{128,256},{256,384},{384,0},{1,129},{129,257},{257,385},{3... | collective-permute-start | bytes 98312 | tf_op jit(solution)/shard_map/ppermute | solution.py:274
  33.6 0.0 collective-permute-done.xleft_ref
  33.7 0.0 collective-permute-done.2.ybelow_hbm
  33.7 0.0 collective-permute-done.3.yabove_hbm
  33.7 0.0 collective-permute-done.4.zbelow_hbm
  33.7 0.0 copy-start
  33.7 0.0 collective-permute-done.5.zabove_hbm
  33.7 0.5 copy-done.5
  34.3 0.0 copy-done.2
  34.3 0.0 copy-done.3
  34.3 0.1 copy-done
  34.4 0.6 copy-done.1
  35.0 16.1 %cells.1 = (f32[32,64,128]{2,1,0:T(8,128)}, f32[32,8,128]{2,1,0:T(8,128)}) custom-call(s32[1]{0:T(128)S(6)} %copy.7.first_ref, s32[1]{0:T(128)S(6)} %copy.8.beyond_ref, bf16[48,128]{1,0:T(8,128)(2,1)} %constant.2.clone.c_ref, f32[4,2048]{1,0:T(4,128)} %get-tuple-element.13.xlo_ref, f32[4,2048]{1,0:T(4,128)} %get-tuple-element.14.xhi_ref, ...), custom_call_target="tpu_custom_call" | custom-call | tf_op jit(solution)/shard_map/cells/pallas_call | solution.py:226
  51.1 14.9 %all_to_all.10.a_ref = f32[32,8,128]{2,1,0:T(8,128)} all-to-all(f32[32,8,128]{2,1,0:T(8,128)} %get-tuple-element.20), channel_id=1, replica_groups=mesh['gx_0'=2,'gx_1'=2,'gy'=16,'gz_0'=2,'gz_1'=4] {'gx_0','gx_1','gz_0',..., dimensions={0} | all-to-all | bytes 262144 | tf_op jit(solution)/shard_map/all_to_all | solution.py:288
  65.9 1.6 %merge.1 = f32[16,8,128]{2,1,0:T(8,128)} custom-call(f32[32,8,128]{2,1,0:T(8,128)} %all_to_all.10.a_ref), custom_call_target="tpu_custom_call" | custom-call | tf_op jit(solution)/shard_map/merge/pallas_call | solution.py:289
  67.5 20.3 %all_to_all.11.a_ref = f32[16,8,128]{2,1,0:T(8,128)} all-to-all(f32[16,8,128]{2,1,0:T(8,128)} %merge.1), channel_id=1, replica_groups=mesh['gx_0'=2,'gx_1'=2,'gy'=16,'gz_0'=2,'gz_1'=4] {'gy'}, dimensions={0} | all-to-all | bytes 131072 | tf_op jit(solution)/shard_map/all_to_all | solution.py:294
  87.8 1.5 %final.1 = (f32[2,128]{1,0:T(2,128)}, f32[4]{0:T(128)}) custom-call(s32[1]{0:T(128)S(6)} %copy.7.first_ref, s32[1]{0:T(128)S(6)} %copy.8.beyond_ref, f32[16,8,128]{2,1,0:T(8,128)} %all_to_all.11.a_ref), custom_call_target="tpu_custom_call" | custom-call | tf_op jit(solution)/shard_map/final/pallas_call | solution.py:297
  (6 shorter events, 0.0 us)
Async XLA Ops:
  2.9 30.8 %collective-permute-start.4 = (f32[4,64,128]{2,1,0:T(8,128)}, f32[4,64,128]{2,1,0:T(8,128)S(1)}, u32[]{:S(2)}, u32[]{:S(2)}) collective-permute-start(f32[4,64,128]{2,1,0:T(8,128)} %get-tuple-element.17), channel_id=1, source_target_pairs={{0,1},{1,2},{2,3},{3,4},{4,5},{5,6},{6,7},{7,0},{8,9},{9,10},{10,1... | collective-permute-start | bytes 393224 | tf_op jit(solution)/shard_map/ppermute | solution.py:274
  6.8 26.9 %collective-permute-start.5 = (f32[4,64,128]{2,1,0:T(8,128)}, f32[4,64,128]{2,1,0:T(8,128)S(1)}, u32[]{:S(2)}, u32[]{:S(2)}) collective-permute-start(f32[4,64,128]{2,1,0:T(8,128)} %get-tuple-element.18), channel_id=1, source_target_pairs={{0,7},{1,0},{2,1},{3,2},{4,3},{5,4},{6,5},{7,6},{8,15},{9,8},{10,9... | collective-permute-start | bytes 393224 | tf_op jit(solution)/shard_map/ppermute | solution.py:274
  11.0 16.3 %collective-permute-start.1 = (f32[4,2048]{1,0:T(4,128)}, f32[4,2048]{1,0:T(4,128)S(1)}, u32[]{:S(2)}, u32[]{:S(2)}) collective-permute-start(f32[4,2048]{1,0:T(4,128)} %get-tuple-element.13.xlo_ref), channel_id=1, source_target_pairs={{0,384},{128,0},{256,128},{384,256},{1,385},{129,1},{257,129},{385... | collective-permute-start | bytes 98312 | tf_op jit(solution)/shard_map/ppermute | solution.py:274
  19.6 14.1 %collective-permute-start.2 = (f32[32,4,128]{2,1,0:T(4,128)}, f32[32,4,128]{2,1,0:T(4,128)S(1)}, u32[]{:S(2)}, u32[]{:S(2)}) collective-permute-start(f32[32,4,128]{2,1,0:T(4,128)} %get-tuple-element.15), channel_id=1, source_target_pairs={{0,8},{8,16},{16,24},{24,32},{32,40},{40,48},{48,56},{56,64},{64,7... | collective-permute-start | bytes 196616 | tf_op jit(solution)/shard_map/ppermute | solution.py:274
  21.5 12.2 %collective-permute-start.3 = (f32[32,4,128]{2,1,0:T(4,128)}, f32[32,4,128]{2,1,0:T(4,128)S(1)}, u32[]{:S(2)}, u32[]{:S(2)}) collective-permute-start(f32[32,4,128]{2,1,0:T(4,128)} %get-tuple-element.16), channel_id=1, source_target_pairs={{0,120},{8,0},{16,8},{24,16},{32,24},{40,32},{48,40},{56,48},{64,5... | collective-permute-start | bytes 196616 | tf_op jit(solution)/shard_map/ppermute | solution.py:274
  27.3 6.4 %copy-start.4 = (f32[4,2048]{1,0:T(4,128)}, f32[4,2048]{1,0:T(4,128)S(1)}, u32[]{:S(2)}) copy-start(f32[4,2048]{1,0:T(4,128)S(1)} %collective-permute-done.1.xright_ref) | copy-start | bytes 98308
  27.3 6.3 %collective-permute-start = (f32[4,2048]{1,0:T(4,128)}, f32[4,2048]{1,0:T(4,128)S(1)}, u32[]{:S(2)}, u32[]{:S(2)}) collective-permute-start(f32[4,2048]{1,0:T(4,128)} %get-tuple-element.14.xhi_ref), channel_id=1, source_target_pairs={{0,128},{128,256},{256,384},{384,0},{1,129},{129,257},{257,385},{3... | collective-permute-start | bytes 98312 | tf_op jit(solution)/shard_map/ppermute | solution.py:274
  33.6 0.6 copy-start.5
  33.7 0.6 copy-start.2
  33.7 0.6 copy-start.3
  33.7 0.7 copy-start
  34.4 0.7 copy-start.1

commit v2 on v1

v2 whole, which is shorter than its diff:
```python
import jax
import jax.numpy as jnp
import numpy as np
from jax import lax
from jax.experimental import pallas as pl
from jax.experimental.pallas import tpu as pltpu
from jax.sharding import Mesh
from jax.sharding import PartitionSpec as P


BINS = 256
GX = ("gx_0", "gx_1")
GZ = ("gz_0", "gz_1")
GX_GZ = ("gx_0", "gx_1", "gz_0", "gz_1")
COEF = tuple(float(np.float32(c)) for c in (0.8, -0.2, 4.0 / 105.0, -1.0 / 280.0))
GRAD_RANGE = 12.0
NZ, NY, NX = 32, 64, 128
ROW = NY + 16
ROUNDER = 49152.0


def split3(a):
    high = a.astype(jnp.bfloat16)
    rest = a - high.astype(jnp.float32)
    mid = rest.astype(jnp.bfloat16)
    low = (rest - mid.astype(jnp.float32)).astype(jnp.bfloat16)
    return high, mid, low


def correction_matrix():
    table = np.zeros((8, NX), np.float32)
    for j in range(4):
        for k in range(1, 5):
            i = NX + j - k
            if i < NX:
                table[j, i] = COEF[k - 1]
            i = k - 4 + j
            if i >= 0:
                table[4 + j, i] = -COEF[k - 1]
    high = table.astype(jnp.bfloat16)
    rest = table - high.astype(np.float32)
    mid = rest.astype(jnp.bfloat16)
    low = (rest - mid.astype(np.float32)).astype(jnp.bfloat16)
    return np.concatenate([high, mid, high, low, mid, high], axis=0)


def in_vmem(a):
    return pltpu.with_memory_space_constraint(a, pltpu.VMEM)


def vmem_out(*shape):
    return pltpu.VMEM(shape, jnp.float32)


VMEM = pl.BlockSpec(memory_space=pltpu.VMEM)
SMEM = pl.BlockSpec(memory_space=pltpu.SMEM)


def pack_kernel(x_ref, copy_ref, xlo_ref, xhi_ref, ylo_ref, yhi_ref, zlo_ref, zhi_ref):
    for i in range(NZ * NY // 128):
        block = x_ref[2 * i : 2 * i + 2].reshape(128, NX)
        turned = block.T
        xlo_ref[:, i * 128 : (i + 1) * 128] = turned[0:4]
        xhi_ref[:, i * 128 : (i + 1) * 128] = turned[NX - 4 :]
    ylo_ref[...] = x_ref[:, 0:4, :]
    yhi_ref[...] = x_ref[:, NY - 4 :, :]
    zlo_ref[...] = x_ref[0:4]
    zhi_ref[...] = x_ref[NZ - 4 :]
    copy_ref[...] = x_ref[...]


def pack(x):
    return pl.pallas_call(
        pack_kernel,
        in_specs=[VMEM],
        out_specs=(VMEM,) * 7,
        out_shape=(
            vmem_out(NZ, NY, NX),
            vmem_out(4, NZ * NY),
            vmem_out(4, NZ * NY),
            vmem_out(NZ, 4, NX),
            vmem_out(NZ, 4, NX),
            vmem_out(4, NY, NX),
            vmem_out(4, NY, NX),
        ),
        name="pack",
    )(x)


def stencil(pairs):
    total = None
    for c, (after, before) in zip(COEF, pairs):
        term = c * (after - before)
        total = term if total is None else total + term
    return total


def xz_kernel(c_ref, x_ref, xlo_ref, xhi_ref, xleft_ref, xright_ref, zbelow_ref, zabove_ref, out_ref, corr_ref):
    for i in range(NZ * NY // 128):
        cut = slice(i * 128, (i + 1) * 128)
        delta = jnp.concatenate(
            [xright_ref[:, cut] - xlo_ref[:, cut], xleft_ref[:, cut] - xhi_ref[:, cut]], axis=0
        )
        h, m, l = split3(delta)
        left = jnp.concatenate([h, h, m, h, m, l], axis=0)
        corr_ref[2 * i : 2 * i + 2] = lax.dot_general(
            left, c_ref[...], (((0,), (0,)), ((), ())), preferred_element_type=jnp.float32
        ).reshape(2, NY, NX)

    def plane(z, fetch):
        center = x_ref[z]
        gx = stencil(
            [(pltpu.roll(center, NX - k, 1), pltpu.roll(center, k, 1)) for k in range(1, 5)]
        )
        gx = gx + corr_ref[z]
        gz = stencil([(fetch(k), fetch(-k)) for k in range(1, 5)])
        out_ref[z] = gx * gx + gz * gz

    for z in (0, 1, 2, 3, NZ - 4, NZ - 3, NZ - 2, NZ - 1):

        def fetch(k):
            at = z + k
            if at < 0:
                return zbelow_ref[at + 4]
            if at >= NZ:
                return zabove_ref[at - NZ]
            return x_ref[at]

        plane(z, fetch)

    def step(z, carry):
        plane(z, lambda k: x_ref[z + k])
        return carry

    lax.fori_loop(4, NZ - 4, step, 0, unroll=4)


def xz_squares(x, edges, halos):
    args = [correction_matrix()] + [in_vmem(a) for a in (x, *edges, *halos)]
    return pl.pallas_call(
        xz_kernel,
        in_specs=[VMEM] * 8,
        out_specs=VMEM,
        out_shape=vmem_out(NZ, NY, NX),
        scratch_shapes=[pltpu.VMEM((NZ, NY, NX), jnp.float32)],
        name="xz",
    )(*args)


def cells_kernel(
    first_ref, beyond_ref, x_ref, square_ref, ybelow_ref, yabove_ref,
    mag_ref, red_ref,
    rows_ref, cell0_ref, cell1_ref, stat_ref,
):
    pl.run_scoped(
        lambda *accs: cells_body(
            first_ref, beyond_ref, x_ref, square_ref, ybelow_ref, yabove_ref,
            mag_ref, red_ref,
            rows_ref, cell0_ref, cell1_ref, stat_ref, *accs,
        ),
        pltpu.ACC(mxu_id=0)((256, 256), jnp.float32),
        pltpu.ACC(mxu_id=1)((256, 256), jnp.float32),
    )


def cells_body(
    first_ref, beyond_ref, x_ref, square_ref, ybelow_ref, yabove_ref,
    mag_ref, red_ref,
    rows_ref, cell0_ref, cell1_ref, stat_ref, acc0_ref, acc1_ref,
):
    cell_refs = (cell0_ref, cell1_ref)
    acc_refs = (acc0_ref, acc1_ref)
    stat_ref[0] = jnp.zeros((8, NX), jnp.float32)
    stat_ref[1] = jnp.full((8, NX), -3.0e38, jnp.float32)
    stat_ref[2] = jnp.full((8, NX), 3.0e38, jnp.float32)
    before = first_ref[0].astype(jnp.float32) - 1.0
    beyond = beyond_ref[0].astype(jnp.float32)
    ids = lax.broadcasted_iota(jnp.int32, (16, NX), 0).astype(jnp.float32).astype(jnp.bfloat16)
    one = jnp.ones((16, NX), jnp.bfloat16)
    zero = jnp.zeros((16, NX), jnp.bfloat16)

    def cells(z, slot):
        cell_ref = cell_refs[slot]
        base = (z % 2) * ROW
        rows_ref[pl.ds(pl.multiple_of(base + 8, 8), NY), :] = x_ref[z]
        rows_ref[pl.ds(base + 4, 4), :] = ybelow_ref[z]
        rows_ref[pl.ds(base + 8 + NY, 4), :] = yabove_ref[z]

        def at(offset):
            return rows_ref[pl.ds(base + 8 + offset, NY), :]

        gy = stencil([(at(k), at(-k)) for k in range(1, 5)])
        norm = square_ref[z] + gy * gy + 1.0
        mag = norm * lax.rsqrt(norm) - 1.0
        mag_ref[z] = mag
        place = jnp.clip(mag * (BINS / GRAD_RANGE), 0.5, BINS - 0.5) - 0.5
        low = jnp.minimum(jnp.floor(place), BINS - 2.0)
        frac = place - low
        weight = jnp.clip(jnp.minimum(place - before, beyond - place), 0.0, 1.0)
        parts = lambda a: a.reshape(NY // 8, 8, NX)
        stat_ref[0] += jnp.sum(parts(weight * mag), axis=0)
        stat_ref[1] = jnp.maximum(stat_ref[1], jnp.max(parts(weight * mag), axis=0))
        stat_ref[2] = jnp.minimum(
            stat_ref[2], jnp.min(parts(mag + GRAD_RANGE * (1.0 - weight)), axis=0)
        )
        coarse = jnp.floor(low * 0.0625)
        frac_high = (frac + ROUNDER) - ROUNDER
        cell_ref[0] = coarse
        cell_ref[1] = low - 16.0 * coarse
        cell_ref[2] = frac_high
        cell_ref[3] = frac - frac_high

    def hist(slot):
        cell_ref = cell_refs[slot]

        def row(q, r):
            return jnp.broadcast_to(cell_ref[q, r : r + 1, :], (16, NX)).astype(jnp.bfloat16)

        for q in range(4):
            left, right = [], []
            for g in range(8):
                sides = []
                for r in (16 * q + 2 * g, 16 * q + 2 * g + 1):
                    coarse = row(0, r) == ids
                    finer = row(1, r) == ids
                    sides.append(
                        (
                            jnp.where(coarse, one, zero),
                            jnp.where(coarse, row(2, r), zero),
                            jnp.where(finer, one, zero),
                            jnp.where(finer, row(3, r), zero),
                        )
                    )
                joined = [jnp.concatenate(pair, axis=1) for pair in zip(*sides)]
                left += joined[:2]
                right += joined[2:]
            mxu = q % 2
            pltpu.matmul_push_rhs(jnp.concatenate(right, axis=0), q // 2, mxu, transpose=True)
            pltpu.matmul_acc_lhs(acc_refs[mxu], jnp.concatenate(left, axis=0), load_staged_rhs=q // 2)

    cells(0, 0)

    def step(i, carry):
        hist(0)
        cells(2 * i + 1, 1)
        hist(1)
        cells(2 * i + 2, 0)
        return carry

    lax.fori_loop(0, NZ // 2 - 1, step, 0)
    hist(0)
    cells(NZ - 1, 1)
    hist(1)

    both = pltpu.matmul_pop(acc0_ref) + pltpu.matmul_pop(acc1_ref)
    lane = lax.broadcasted_iota(jnp.int32, (32, NX), 1)
    total = jnp.zeros((32, NX), jnp.float32)
    for g in range(8):
        part = both[g * 32 : (g + 1) * 32, (g // 4) * NX : (g // 4 + 1) * NX]
        total = total + jnp.where(lane // 32 == g % 4, part, 0.0)
    for shift in (64, 32):
        total = total + pltpu.roll(total, shift, 1)
    lane = lax.broadcasted_iota(jnp.int32, (16, NX), 1)
    sub = lax.broadcasted_iota(jnp.int32, (16, NX), 0)
    plain = total[0:16]
    upper = total[16:32] + pltpu.roll(plain, NX - 16, 1)

    def repeated(a):
        a = jnp.where(lane % 32 < 16, a, 0.0)
        return a + pltpu.roll(a, 16, 1)

    plain = repeated(plain)
    upper = repeated(upper)
    beside = pltpu.roll(upper, 1, 1)
    carried = jnp.where(sub == 0, 0.0, pltpu.roll(beside, 1, 0))
    counts = plain - upper + jnp.where(lane % 16 == 0, carried, beside)
    tops = [
        jnp.sum(jnp.where(sub == 8 * h + lane // 16, counts, 0.0), axis=0, keepdims=True)
        for h in range(2)
    ]
    tile = jnp.concatenate(
        tops
        + [
            jnp.sum(stat_ref[0], axis=0, keepdims=True),
            jnp.max(stat_ref[1], axis=0, keepdims=True),
            jnp.min(stat_ref[2], axis=0, keepdims=True),
            jnp.zeros((3, NX), jnp.float32),
        ],
        axis=0,
    )
    red_ref[...] = jnp.broadcast_to(tile[None], red_ref.shape)


def cells(x, squares, halos, first, beyond, peers):
    args = [in_vmem(a) for a in (x, squares, *halos)]
    return pl.pallas_call(
        cells_kernel,
        in_specs=[SMEM, SMEM] + [VMEM] * 4,
        out_specs=(VMEM, VMEM),
        out_shape=(vmem_out(NZ, NY, NX), vmem_out(peers, 8, NX)),
        scratch_shapes=[
            pltpu.VMEM((2 * ROW, NX), jnp.float32),
            pltpu.VMEM((4, NY, NX), jnp.float32),
            pltpu.VMEM((4, NY, NX), jnp.float32),
            pltpu.VMEM((3, 8, NX), jnp.float32),
        ],
        input_output_aliases={3: 0},
        name="cells",
    )(first, beyond, *args)


def merged(a):
    summed = jnp.sum(a[:, 0:3, :], axis=0)
    high = jnp.max(a[:, 3:4, :], axis=0)
    low = jnp.min(a[:, 4:5, :], axis=0)
    return summed, high, low


def merge_kernel(a_ref, out_ref):
    summed, high, low = merged(a_ref)
    tile = jnp.concatenate([summed, high, low, jnp.zeros((3, NX), jnp.float32)], axis=0)
    out_ref[...] = jnp.broadcast_to(tile[None], out_ref.shape)


def merge(a, peers):
    return pl.pallas_call(
        merge_kernel,
        in_specs=[VMEM],
        out_specs=VMEM,
        out_shape=vmem_out(peers, 8, NX),
        name="merge",
    )(in_vmem(a))


def final_kernel(first_ref, beyond_ref, a_ref, hist_ref, stats_ref):
    summed, high, low = merged(a_ref)
    total_cells = 134217728.0
    counts = summed[0:2]
    hist_ref[...] = counts * (BINS / total_cells)
    bins = lax.broadcasted_iota(jnp.int32, (2, NX), 0) * NX + lax.broadcasted_iota(jnp.int32, (2, NX), 1)
    inside = (bins >= first_ref[0]) & (bins < beyond_ref[0])
    stats_ref[0] = jnp.min(low)
    stats_ref[1] = jnp.max(high)
    stats_ref[2] = jnp.sum(summed[2:3]) / total_cells
    stats_ref[3] = jnp.sum(jnp.where(inside, counts, 0.0)) / total_cells


def final(a, first, beyond):
    hist, stats = pl.pallas_call(
        final_kernel,
        in_specs=[SMEM, SMEM, VMEM],
        out_specs=(VMEM, SMEM),
        out_shape=(
            jax.ShapeDtypeStruct((2, NX), jnp.float32),
            jax.ShapeDtypeStruct((4,), jnp.float32),
        ),
        name="final",
    )(first, beyond, in_vmem(a))
    return hist.reshape(BINS), stats


def shifted(part, axis, step):
    count = lax.axis_size(axis)
    return lax.ppermute(part, axis, [(i, (i + step) % count) for i in range(count)])


def on_device(x, first, beyond):
    x, xlo, xhi, ylo, yhi, zlo, zhi = pack(x)
    xleft = shifted(xhi, GX, 1)
    xright = shifted(xlo, GX, -1)
    zbelow = shifted(zhi, GZ, 1)
    zabove = shifted(zlo, GZ, -1)
    ybelow = shifted(yhi, "gy", 1)
    yabove = shifted(ylo, "gy", -1)
    squares = xz_squares(x, (xlo, xhi), (xleft, xright, zbelow, zabove))
    mag, red = cells(x, squares, (ybelow, yabove), first, beyond, lax.axis_size(GX_GZ))
    red = lax.all_to_all(red, GX_GZ, 0, 0)
    red = merge(red, lax.axis_size("gy"))
    red = lax.all_to_all(red, "gy", 0, 0)
    hist, stats = final(red, first, beyond)
    return mag, hist, stats


def solution(mesh):
    finer = Mesh(
        mesh.devices.reshape(2, 2, mesh.shape["gy"], 2, 4), ("gx_0", "gx_1", "gy", "gz_0", "gz_1")
    )
    return jax.shard_map(
        on_device,
        mesh=finer,
        in_specs=(P(GZ, "gy", GX), P(), P()),
        out_specs=(P(GZ, "gy", GX), P(), P()),
        check_vma=False,
    )
```

time: 89.9 us -> 79 us (0.88)
  blocking collectives: 35.2 us -> 13.1 us
  waiting for transfers between devices: 0.04 us -> 10.6 us
  starting transfers between devices: 29.4 us -> 38 us
  Pallas kernels: 21.4 us -> 13.8 us
    all_to_all x1 -> x0, blocking collectives: 20.3 us -> none  [on_device(): red = lax.all_to_all(red, 'gy', 0, 0)]
    all_to_all x0 -> x1, waiting for transfers between devices: none -> 10.6 us  [on_device(): red = lax.all_to_all(red, 'gy', 0, 0)]
    all_to_all x0 -> x1, starting transfers between devices: none -> 8.65 us  [on_device(): red = lax.all_to_all(red, 'gy', 0, 0)]
    pallas_call x4 -> x5, Pallas kernels: 21.4 us -> 13.8 us  [the longest x1 7.28 us: cells(): pl.pallas_call(cells_kernel, in_specs=[SMEM, SMEM] + [VMEM] * 4, out_spec...]
    all_to_all x1, blocking collectives: 14.9 us -> 13.1 us  [on_device(): red = lax.all_to_all(red, GX_GZ, 0, 0)]
  transfers between devices with their start and end apart: 6 -> 7, of which waited for: 0 -> 1; matrix products, arithmetic and copies ran while one was open for 0% -> 1% of each run, Pallas kernels for 0% -> 5%
where the time goes in v2:
time: 79 us; the launch traced here: 78.6 us
  starting transfers between devices  38 us (48%)
  Pallas kernels  13.8 us (17%)
  blocking collectives  13.1 us (17%)
  waiting for transfers between devices  10.6 us (13%)
  between operations  2.05 us (3%)
  local copies, waits for them, and re-layouts  0.97 us (1%)
    ppermute x6, starting transfers between devices, shifted(): lax.ppermute(part, axis, [(i, (i + step) % count) for i in range(count)])  29.4 us
    all_to_all x1, blocking collectives, on_device(): red = lax.all_to_all(red, GX_GZ, 0, 0)  13.1 us
    all_to_all x1, waiting for transfers between devices, on_device(): red = lax.all_to_all(red, 'gy', 0, 0)  10.6 us
    all_to_all x1, starting transfers between devices, on_device(): red = lax.all_to_all(red, 'gy', 0, 0)  8.65 us
    pallas_call x1, Pallas kernels, cells(): pl.pallas_call(cells_kernel, in_specs=[SMEM, SMEM] + [VMEM] * 4, out_spec...  7.28 us
    pallas_call x1, Pallas kernels, xz_squares(): pl.pallas_call(xz_kernel, in_specs=[VMEM] * 8, out_specs=VMEM, out_shape=...  3.56 us
    pallas_call x1, Pallas kernels, pack(): pl.pallas_call(pack_kernel, in_specs=[VMEM], out_specs=(VMEM,) * 7, out_s...  1.64 us
  transfers between devices with their start and end apart: 7, of which 1 were waited for; matrix products, arithmetic and copies ran while one was open for 1% of the time, Pallas kernels for 5%

profile of v2, /device:TPU:1, one launch (start us, length us, event | category | flops | bytes accessed | tf_op | source)
XLA Modules:
  0.0 78.6 jit_solution(204711361526805314)
XLA Ops:
  0.6 1.6 %pack.1 = (f32[32,64,128]{2,1,0:T(8,128)S(1)}, f32[4,2048]{1,0:T(4,128)S(1)}, f32[4,2048]{1,0:T(4,128)S(1)}, f32[32,4,128]{2,1,0:T(4,128)S(1)}, f32[32,4,128]{2,...) custom-call(f32[32,64,128]{2,1,0:T(8,128)} %x_ref.1), custom_call_target="tpu_custom_call" | custom-call | tf_op jit(solution)/shard_map/pack/pallas_call | solution.py:73
  2.3 3.9 %collective-permute-start.2 = (f32[4,64,128]{2,1,0:T(8,128)S(1)}, f32[4,64,128]{2,1,0:T(8,128)S(1)}, u32[]{:S(2)}, u32[]{:S(2)}) collective-permute-start(f32[4,64,128]{2,1,0:T(8,128)S(1)} %get-tuple-element.17), channel_id=1, source_target_pairs={{0,1},{1,2},{2,3},{3,4},{4,5},{5,6},{6,7},{7,0},{8,9},{9,10},{10,1... | collective-permute-start | bytes 393224 | tf_op jit(solution)/shard_map/ppermute | solution.py:364
  6.2 4.2 %collective-permute-start.3 = (f32[4,64,128]{2,1,0:T(8,128)S(1)}, f32[4,64,128]{2,1,0:T(8,128)S(1)}, u32[]{:S(2)}, u32[]{:S(2)}) collective-permute-start(f32[4,64,128]{2,1,0:T(8,128)S(1)} %get-tuple-element.18), channel_id=1, source_target_pairs={{0,7},{1,0},{2,1},{3,2},{4,3},{5,4},{6,5},{7,6},{8,15},{9,8},{10,9... | collective-permute-start | bytes 393224 | tf_op jit(solution)/shard_map/ppermute | solution.py:364
  10.4 8.6 %collective-permute-start.1 = (f32[4,2048]{1,0:T(4,128)S(1)}, f32[4,2048]{1,0:T(4,128)S(1)}, u32[]{:S(2)}, u32[]{:S(2)}) collective-permute-start(f32[4,2048]{1,0:T(4,128)S(1)} %get-tuple-element.15.xlo_ref), channel_id=1, source_target_pairs={{0,384},{128,0},{256,128},{384,256},{1,385},{129,1},{257,129},{385... | collective-permute-start | bytes 98312 | tf_op jit(solution)/shard_map/ppermute | solution.py:364
  19.0 1.9 %collective-permute-start.4 = (f32[32,4,128]{2,1,0:T(4,128)S(1)}, f32[32,4,128]{2,1,0:T(4,128)S(1)}, u32[]{:S(2)}, u32[]{:S(2)}) collective-permute-start(f32[32,4,128]{2,1,0:T(4,128)S(1)} %get-tuple-element.19), channel_id=1, source_target_pairs={{0,8},{8,16},{16,24},{24,32},{32,40},{40,48},{48,56},{56,64},{64,7... | collective-permute-start | bytes 196616 | tf_op jit(solution)/shard_map/ppermute | solution.py:364
  20.9 5.8 %collective-permute-start.5 = (f32[32,4,128]{2,1,0:T(4,128)S(1)}, f32[32,4,128]{2,1,0:T(4,128)S(1)}, u32[]{:S(2)}, u32[]{:S(2)}) collective-permute-start(f32[32,4,128]{2,1,0:T(4,128)S(1)} %get-tuple-element.20), channel_id=1, source_target_pairs={{0,120},{8,0},{16,8},{24,16},{32,24},{40,32},{48,40},{56,48},{64,5... | collective-permute-start | bytes 196616 | tf_op jit(solution)/shard_map/ppermute | solution.py:364
  26.7 0.0 collective-permute-done.1.xright_ref
  26.7 5.0 %collective-permute-start = (f32[4,2048]{1,0:T(4,128)S(1)}, f32[4,2048]{1,0:T(4,128)S(1)}, u32[]{:S(2)}, u32[]{:S(2)}) collective-permute-start(f32[4,2048]{1,0:T(4,128)S(1)} %get-tuple-element.16.xhi_ref), channel_id=1, source_target_pairs={{0,128},{128,256},{256,384},{384,0},{1,129},{129,257},{257,385},{3... | collective-permute-start | bytes 98312 | tf_op jit(solution)/shard_map/ppermute | solution.py:364
  33.0 0.0 collective-permute-done.xleft_ref
  33.0 0.0 collective-permute-done.2.zbelow_ref
  33.0 0.0 collective-permute-done.3.zabove_ref
  33.1 3.6 %xz.1.square_ref = f32[32,64,128]{2,1,0:T(8,128)S(1)} custom-call(bf16[48,128]{1,0:T(8,128)(2,1)} %constant.2.clone.c_ref, f32[32,64,128]{2,1,0:T(8,128)S(1)} %get-tuple-element.14.x_ref, f32[4,2048]{1,0:T(4,128)S(1)} %get-tuple-element.15.xlo_ref, f32[4,2048]{1,0:T(4,128)S(1)} %get-tuple-element.16.xhi_ref, f32[4,2048]{1,0:T(4,128)S(1)} %collective-permute-done.xleft_ref, ...), custom_call_target="tpu_custom_call" | custom-call | tf_op jit(solution)/shard_map/xz/pallas_call | solution.py:140
  36.6 0.0 collective-permute-done.4.ybelow_ref
  36.6 0.0 collective-permute-done.5.yabove_ref
  36.6 7.3 %cells.1 = (f32[32,64,128]{2,1,0:T(8,128)S(1)}, f32[32,8,128]{2,1,0:T(8,128)S(1)}) custom-call(s32[1]{0:T(128)S(6)} %copy.10.first_ref, s32[1]{0:T(128)S(6)} %copy.11.beyond_ref, f32[32,64,128]{2,1,0:T(8,128)S(1)} %get-tuple-element.14.x_ref, f32[32,64,128]{2,1,0:T(8,128)S(1)} %xz.1.square_ref, ...), custom_call_target="tpu_custom_call", output_to_operand_aliasing={{0}: (3, {})} | custom-call | tf_op jit(solution)/shard_map/cells/pallas_call | solution.py:296
  43.9 13.1 %all_to_all.10.a_ref = f32[32,8,128]{2,1,0:T(8,128)S(1)} all-to-all(f32[32,8,128]{2,1,0:T(8,128)S(1)} %get-tuple-element.22), channel_id=1, replica_groups=mesh['gx_0'=2,'gx_1'=2,'gy'=16,'gz_0'=2,'gz_1'=4] {'gx_0','gx_1','gz_0',..., dimensions={0} | all-to-all | bytes 262144 | tf_op jit(solution)/shard_map/all_to_all | solution.py:377
  57.0 0.7 merge.1
  57.7 8.7 %all-to-all-start.1 = ((f32[16,8,128]{2,1,0:T(8,128)}), f32[16,8,128]{2,1,0:T(8,128)S(1)}, u32[]{:S(2)}, u32[]{:S(2)}) async-start(f32[16,8,128]{2,1,0:T(8,128)} %merge.1), calls=%async_computation.1 | async-start | bytes 131072 | tf_op jit(solution)/shard_map/all_to_all | solution.py:379
  66.3 1.0 %copy.9 = f32[32,64,128]{2,1,0:T(8,128)} copy(f32[32,64,128]{2,1,0:T(8,128)S(1)} %get-tuple-element.25) | data formatting | bytes 2097152
  67.3 10.6 %all-to-all-done.1.a_ref = f32[16,8,128]{2,1,0:T(8,128)S(1)} async-done(((f32[16,8,128]{2,1,0:T(8,128)}), f32[16,8,128]{2,1,0:T(8,128)S(1)}, u32[]{:S(2)}, u32[]{:S(2)}) %all-to-all-start.1) | async-done | bytes 65568 | tf_op jit(solution)/shard_map/all_to_all | solution.py:379
  77.9 0.7 final.1
Async XLA Ops:
  2.3 30.8 %collective-permute-start.2 = (f32[4,64,128]{2,1,0:T(8,128)S(1)}, f32[4,64,128]{2,1,0:T(8,128)S(1)}, u32[]{:S(2)}, u32[]{:S(2)}) collective-permute-start(f32[4,64,128]{2,1,0:T(8,128)S(1)} %get-tuple-element.17), channel_id=1, source_target_pairs={{0,1},{1,2},{2,3},{3,4},{4,5},{5,6},{6,7},{7,0},{8,9},{9,10},{10,1... | collective-permute-start | bytes 393224 | tf_op jit(solution)/shard_map/ppermute | solution.py:364
  6.2 26.8 %collective-permute-start.3 = (f32[4,64,128]{2,1,0:T(8,128)S(1)}, f32[4,64,128]{2,1,0:T(8,128)S(1)}, u32[]{:S(2)}, u32[]{:S(2)}) collective-permute-start(f32[4,64,128]{2,1,0:T(8,128)S(1)} %get-tuple-element.18), channel_id=1, source_target_pairs={{0,7},{1,0},{2,1},{3,2},{4,3},{5,4},{6,5},{7,6},{8,15},{9,8},{10,9... | collective-permute-start | bytes 393224 | tf_op jit(solution)/shard_map/ppermute | solution.py:364
  10.4 16.3 %collective-permute-start.1 = (f32[4,2048]{1,0:T(4,128)S(1)}, f32[4,2048]{1,0:T(4,128)S(1)}, u32[]{:S(2)}, u32[]{:S(2)}) collective-permute-start(f32[4,2048]{1,0:T(4,128)S(1)} %get-tuple-element.15.xlo_ref), channel_id=1, source_target_pairs={{0,384},{128,0},{256,128},{384,256},{1,385},{129,1},{257,129},{385... | collective-permute-start | bytes 98312 | tf_op jit(solution)/shard_map/ppermute | solution.py:364
  19.0 17.6 %collective-permute-start.4 = (f32[32,4,128]{2,1,0:T(4,128)S(1)}, f32[32,4,128]{2,1,0:T(4,128)S(1)}, u32[]{:S(2)}, u32[]{:S(2)}) collective-permute-start(f32[32,4,128]{2,1,0:T(4,128)S(1)} %get-tuple-element.19), channel_id=1, source_target_pairs={{0,8},{8,16},{16,24},{24,32},{32,40},{40,48},{48,56},{56,64},{64,7... | collective-permute-start | bytes 196616 | tf_op jit(solution)/shard_map/ppermute | solution.py:364
  20.9 15.7 %collective-permute-start.5 = (f32[32,4,128]{2,1,0:T(4,128)S(1)}, f32[32,4,128]{2,1,0:T(4,128)S(1)}, u32[]{:S(2)}, u32[]{:S(2)}) collective-permute-start(f32[32,4,128]{2,1,0:T(4,128)S(1)} %get-tuple-element.20), channel_id=1, source_target_pairs={{0,120},{8,0},{16,8},{24,16},{32,24},{40,32},{48,40},{56,48},{64,5... | collective-permute-start | bytes 196616 | tf_op jit(solution)/shard_map/ppermute | solution.py:364
  26.7 6.3 %collective-permute-start = (f32[4,2048]{1,0:T(4,128)S(1)}, f32[4,2048]{1,0:T(4,128)S(1)}, u32[]{:S(2)}, u32[]{:S(2)}) collective-permute-start(f32[4,2048]{1,0:T(4,128)S(1)} %get-tuple-element.16.xhi_ref), channel_id=1, source_target_pairs={{0,128},{128,256},{256,384},{384,0},{1,129},{129,257},{257,385},{3... | collective-permute-start | bytes 98312 | tf_op jit(solution)/shard_map/ppermute | solution.py:364
  57.7 20.2 %all-to-all-start.1 = ((f32[16,8,128]{2,1,0:T(8,128)}), f32[16,8,128]{2,1,0:T(8,128)S(1)}, u32[]{:S(2)}, u32[]{:S(2)}) async-start(f32[16,8,128]{2,1,0:T(8,128)} %merge.1), calls=%async_computation.1 | async-start | bytes 131072 | tf_op jit(solution)/shard_map/all_to_all | solution.py:379

commit v3 on v2

--- a/solution.py
+++ b/solution.py
@@ -56,23 +56,42 @@
 SMEM = pl.BlockSpec(memory_space=pltpu.SMEM)
 
 
-def pack_kernel(x_ref, copy_ref, xlo_ref, xhi_ref, ylo_ref, yhi_ref, zlo_ref, zhi_ref):
-    for i in range(NZ * NY // 128):
-        block = x_ref[2 * i : 2 * i + 2].reshape(128, NX)
-        turned = block.T
-        xlo_ref[:, i * 128 : (i + 1) * 128] = turned[0:4]
-        xhi_ref[:, i * 128 : (i + 1) * 128] = turned[NX - 4 :]
-    ylo_ref[...] = x_ref[:, 0:4, :]
-    yhi_ref[...] = x_ref[:, NY - 4 :, :]
-    zlo_ref[...] = x_ref[0:4]
-    zhi_ref[...] = x_ref[NZ - 4 :]
-    copy_ref[...] = x_ref[...]
+def odd(axis):
+    return lax.axis_index(axis) % 2 == 1
+
+
+def pack_kernel(x_hbm, x_ref, xa_ref, xb_ref, ya_ref, yb_ref, za_ref, zb_ref, sems):
+    count = 4
+    planes = NZ // count
+    copies = [
+        pltpu.make_async_copy(
+            x_hbm.at[i * planes : (i + 1) * planes], x_ref.at[i * planes : (i + 1) * planes], sems.at[i]
+        )
+        for i in range(count)
+    ]
+    for copy in copies:
+        copy.start()
+    odd_x, odd_y, odd_z = odd(GX), odd("gy"), odd(GZ)
+    for i in range(count):
+        copies[i].wait()
+        for j in range(i * planes // 2, (i + 1) * planes // 2):
+            turned = x_ref[2 * j : 2 * j + 2].reshape(128, NX).T
+            low, high = turned[0:4], turned[NX - 4 :]
+            xa_ref[:, j * 128 : (j + 1) * 128] = jnp.where(odd_x, low, high)
+            xb_ref[:, j * 128 : (j + 1) * 128] = jnp.where(odd_x, high, low)
+        for z in range(i * planes, (i + 1) * planes):
+            low, high = x_ref[z, 0:4], x_ref[z, NY - 4 :]
+            ya_ref[z] = jnp.where(odd_y, low, high)
+            yb_ref[z] = jnp.where(odd_y, high, low)
+    low, high = x_ref[0:4], x_ref[NZ - 4 :]
+    za_ref[...] = jnp.where(odd_z, low, high)
+    zb_ref[...] = jnp.where(odd_z, high, low)
 
 
 def pack(x):
     return pl.pallas_call(
         pack_kernel,
-        in_specs=[VMEM],
+        in_specs=[pl.BlockSpec(memory_space=pl.ANY)],
         out_specs=(VMEM,) * 7,
         out_shape=(
             vmem_out(NZ, NY, NX),
@@ -83,6 +102,7 @@
             vmem_out(4, NY, NX),
             vmem_out(4, NY, NX),
         ),
+        scratch_shapes=[pltpu.SemaphoreType.DMA((4,))],
         name="pack",
     )(x)
 
@@ -95,11 +115,15 @@
     return total
 
 
-def xz_kernel(c_ref, x_ref, xlo_ref, xhi_ref, xleft_ref, xright_ref, zbelow_ref, zabove_ref, out_ref, corr_ref):
+def xz_kernel(c_ref, x_ref, xa_ref, xb_ref, from_xa_ref, from_xb_ref, from_za_ref, from_zb_ref, out_ref, corr_ref):
+    odd_x, odd_z = odd(GX), odd(GZ)
+
     for i in range(NZ * NY // 128):
         cut = slice(i * 128, (i + 1) * 128)
+        by_a = from_xa_ref[:, cut] - xb_ref[:, cut]
+        by_b = from_xb_ref[:, cut] - xa_ref[:, cut]
         delta = jnp.concatenate(
-            [xright_ref[:, cut] - xlo_ref[:, cut], xleft_ref[:, cut] - xhi_ref[:, cut]], axis=0
+            [jnp.where(odd_x, by_b, by_a), jnp.where(odd_x, by_a, by_b)], axis=0
         )
         h, m, l = split3(delta)
         left = jnp.concatenate([h, h, m, h, m, l], axis=0)
@@ -121,9 +145,9 @@
         def fetch(k):
             at = z + k
             if at < 0:
-                return zbelow_ref[at + 4]
+                return jnp.where(odd_z, from_za_ref[at + 4], from_zb_ref[at + 4])
             if at >= NZ:
-                return zabove_ref[at - NZ]
+                return jnp.where(odd_z, from_zb_ref[at - NZ], from_za_ref[at - NZ])
             return x_ref[at]
 
         plane(z, fetch)
@@ -148,15 +172,15 @@
 
 
 def cells_kernel(
-    first_ref, beyond_ref, x_ref, square_ref, ybelow_ref, yabove_ref,
-    mag_ref, red_ref,
-    rows_ref, cell0_ref, cell1_ref, stat_ref,
+    first_ref, beyond_ref, x_ref, square_ref, from_ya_ref, from_yb_ref,
+    mag_ref, mag_hbm, red_ref,
+    rows_ref, cell0_ref, cell1_ref, stat_ref, sems,
 ):
     pl.run_scoped(
         lambda *accs: cells_body(
-            first_ref, beyond_ref, x_ref, square_ref, ybelow_ref, yabove_ref,
-            mag_ref, red_ref,
-            rows_ref, cell0_ref, cell1_ref, stat_ref, *accs,
+            first_ref, beyond_ref, x_ref, square_ref, from_ya_ref, from_yb_ref,
+            mag_ref, mag_hbm, red_ref,
+            rows_ref, cell0_ref, cell1_ref, stat_ref, sems, *accs,
         ),
         pltpu.ACC(mxu_id=0)((256, 256), jnp.float32),
         pltpu.ACC(mxu_id=1)((256, 256), jnp.float32),
@@ -164,9 +188,9 @@
 
 
 def cells_body(
-    first_ref, beyond_ref, x_ref, square_ref, ybelow_ref, yabove_ref,
-    mag_ref, red_ref,
-    rows_ref, cell0_ref, cell1_ref, stat_ref, acc0_ref, acc1_ref,
+    first_ref, beyond_ref, x_ref, square_ref, from_ya_ref, from_yb_ref,
+    mag_ref, mag_hbm, red_ref,
+    rows_ref, cell0_ref, cell1_ref, stat_ref, sems, acc0_ref, acc1_ref,
 ):
     cell_refs = (cell0_ref, cell1_ref)
     acc_refs = (acc0_ref, acc1_ref)
@@ -175,6 +199,7 @@
     stat_ref[2] = jnp.full((8, NX), 3.0e38, jnp.float32)
     before = first_ref[0].astype(jnp.float32) - 1.0
     beyond = beyond_ref[0].astype(jnp.float32)
+    odd_y = odd("gy")
     ids = lax.broadcasted_iota(jnp.int32, (16, NX), 0).astype(jnp.float32).astype(jnp.bfloat16)
     one = jnp.ones((16, NX), jnp.bfloat16)
     zero = jnp.zeros((16, NX), jnp.bfloat16)
@@ -183,8 +208,9 @@
         cell_ref = cell_refs[slot]
         base = (z % 2) * ROW
         rows_ref[pl.ds(pl.multiple_of(base + 8, 8), NY), :] = x_ref[z]
-        rows_ref[pl.ds(base + 4, 4), :] = ybelow_ref[z]
-        rows_ref[pl.ds(base + 8 + NY, 4), :] = yabove_ref[z]
+        by_a, by_b = from_ya_ref[z], from_yb_ref[z]
+        rows_ref[pl.ds(base + 4, 4), :] = jnp.where(odd_y, by_a, by_b)
+        rows_ref[pl.ds(base + 8 + NY, 4), :] = jnp.where(odd_y, by_b, by_a)
 
         def at(offset):
             return rows_ref[pl.ds(base + 8 + offset, NY), :]
@@ -238,6 +264,9 @@
             pltpu.matmul_push_rhs(jnp.concatenate(right, axis=0), q // 2, mxu, transpose=True)
             pltpu.matmul_acc_lhs(acc_refs[mxu], jnp.concatenate(left, axis=0), load_staged_rhs=q // 2)
 
+    def written(z, count):
+        return pltpu.make_async_copy(mag_ref.at[pl.ds(z, count)], mag_hbm.at[pl.ds(z, count)], sems.at[0])
+
     cells(0, 0)
 
     def step(i, carry):
@@ -245,11 +274,13 @@
         cells(2 * i + 1, 1)
         hist(1)
         cells(2 * i + 2, 0)
+        written(2 * i, 2).start()
         return carry
 
     lax.fori_loop(0, NZ // 2 - 1, step, 0)
     hist(0)
     cells(NZ - 1, 1)
+    written(NZ - 2, 2).start()
     hist(1)
 
     both = pltpu.matmul_pop(acc0_ref) + pltpu.matmul_pop(acc1_ref)
@@ -278,47 +309,52 @@
         jnp.sum(jnp.where(sub == 8 * h + lane // 16, counts, 0.0), axis=0, keepdims=True)
         for h in range(2)
     ]
+    high = jnp.max(stat_ref[1], axis=0, keepdims=True)
+    low = jnp.min(stat_ref[2], axis=0, keepdims=True)
+    high = jnp.maximum(high, pltpu.roll(high, NX // 2, 1))
+    low = jnp.minimum(low, pltpu.roll(low, NX // 2, 1))
+    extremes = jnp.where(lane[0:1] < NX // 2, high, low)
     tile = jnp.concatenate(
-        tops
-        + [
-            jnp.sum(stat_ref[0], axis=0, keepdims=True),
-            jnp.max(stat_ref[1], axis=0, keepdims=True),
-            jnp.min(stat_ref[2], axis=0, keepdims=True),
-            jnp.zeros((3, NX), jnp.float32),
-        ],
-        axis=0,
+        tops + [jnp.sum(stat_ref[0], axis=0, keepdims=True), extremes], axis=0
     )
     red_ref[...] = jnp.broadcast_to(tile[None], red_ref.shape)
-
-
-def cells(x, squares, halos, first, beyond, peers):
+    written(0, NZ).wait()
+
+
+def cells(first, beyond, x, squares, halos, peers):
     args = [in_vmem(a) for a in (x, squares, *halos)]
-    return pl.pallas_call(
+    _, mag, red = pl.pallas_call(
         cells_kernel,
         in_specs=[SMEM, SMEM] + [VMEM] * 4,
-        out_specs=(VMEM, VMEM),
-        out_shape=(vmem_out(NZ, NY, NX), vmem_out(peers, 8, NX)),
+        out_specs=(VMEM, pl.BlockSpec(memory_space=pl.ANY), VMEM),
+        out_shape=(
+            vmem_out(NZ, NY, NX),
+            jax.ShapeDtypeStruct((NZ, NY, NX), jnp.float32),
+            vmem_out(peers, 4, NX),
+        ),
         scratch_shapes=[
             pltpu.VMEM((2 * ROW, NX), jnp.float32),
             pltpu.VMEM((4, NY, NX), jnp.float32),
             pltpu.VMEM((4, NY, NX), jnp.float32),
             pltpu.VMEM((3, 8, NX), jnp.float32),
+            pltpu.SemaphoreType.DMA((1,)),
         ],
         input_output_aliases={3: 0},
         name="cells",
     )(first, beyond, *args)
-
-
-def merged(a):
-    summed = jnp.sum(a[:, 0:3, :], axis=0)
+    return mag, red
+
+
+def merged(a_ref):
+    a = a_ref[...]
+    lane = lax.broadcasted_iota(jnp.int32, (1, NX), 1)
     high = jnp.max(a[:, 3:4, :], axis=0)
-    low = jnp.min(a[:, 4:5, :], axis=0)
-    return summed, high, low
+    low = jnp.min(a[:, 3:4, :], axis=0)
+    return jnp.sum(a[:, 0:3, :], axis=0), jnp.where(lane < NX // 2, high, low)
 
 
 def merge_kernel(a_ref, out_ref):
-    summed, high, low = merged(a_ref)
-    tile = jnp.concatenate([summed, high, low, jnp.zeros((3, NX), jnp.float32)], axis=0)
+    tile = jnp.concatenate(merged(a_ref), axis=0)
     out_ref[...] = jnp.broadcast_to(tile[None], out_ref.shape)
 
 
@@ -327,25 +363,27 @@
         merge_kernel,
         in_specs=[VMEM],
         out_specs=VMEM,
-        out_shape=vmem_out(peers, 8, NX),
+        out_shape=vmem_out(peers, 4, NX),
         name="merge",
     )(in_vmem(a))
 
 
 def final_kernel(first_ref, beyond_ref, a_ref, hist_ref, stats_ref):
-    summed, high, low = merged(a_ref)
+    summed, extremes = merged(a_ref)
     total_cells = 134217728.0
     counts = summed[0:2]
     hist_ref[...] = counts * (BINS / total_cells)
-    bins = lax.broadcasted_iota(jnp.int32, (2, NX), 0) * NX + lax.broadcasted_iota(jnp.int32, (2, NX), 1)
+    lane = lax.broadcasted_iota(jnp.int32, (2, NX), 1)
+    bins = lax.broadcasted_iota(jnp.int32, (2, NX), 0) * NX + lane
     inside = (bins >= first_ref[0]) & (bins < beyond_ref[0])
-    stats_ref[0] = jnp.min(low)
-    stats_ref[1] = jnp.max(high)
+    low_half = lane[0:1] < NX // 2
+    stats_ref[0] = jnp.min(jnp.where(low_half, 3.0e38, extremes))
+    stats_ref[1] = jnp.max(jnp.where(low_half, extremes, -3.0e38))
     stats_ref[2] = jnp.sum(summed[2:3]) / total_cells
     stats_ref[3] = jnp.sum(jnp.where(inside, counts, 0.0)) / total_cells
 
 
-def final(a, first, beyond):
+def final(first, beyond, a):
     hist, stats = pl.pallas_call(
         final_kernel,
         in_specs=[SMEM, SMEM, VMEM],
@@ -359,25 +397,27 @@
     return hist.reshape(BINS), stats
 
 
-def shifted(part, axis, step):
+def swapped(part, axis, side):
     count = lax.axis_size(axis)
-    return lax.ppermute(part, axis, [(i, (i + step) % count) for i in range(count)])
+    pairs = [((i + side) % count, (i + 1 + side) % count) for i in range(0, count, 2)]
+    return lax.ppermute(part, axis, pairs + [(b, a) for a, b in pairs])
+
+
+STARTS = ("x_a", "x_b", "z_a", "z_b", "y_a", "y_b")
 
 
 def on_device(x, first, beyond):
-    x, xlo, xhi, ylo, yhi, zlo, zhi = pack(x)
-    xleft = shifted(xhi, GX, 1)
-    xright = shifted(xlo, GX, -1)
-    zbelow = shifted(zhi, GZ, 1)
-    zabove = shifted(zlo, GZ, -1)
-    ybelow = shifted(yhi, "gy", 1)
-    yabove = shifted(ylo, "gy", -1)
-    squares = xz_squares(x, (xlo, xhi), (xleft, xright, zbelow, zabove))
-    mag, red = cells(x, squares, (ybelow, yabove), first, beyond, lax.axis_size(GX_GZ))
+    x, *sends = pack(x)
+    xa, xb, ya, yb, za, zb = sends
+    got = {}
+    for name, part, axis in zip(STARTS, (xa, xb, za, zb, ya, yb), (GX, GX, GZ, GZ, "gy", "gy")):
+        got[name] = swapped(part, axis, 0 if name[-1] == "a" else 1)
+    squares = xz_squares(x, (xa, xb), [got[name] for name in STARTS[:4]])
+    mag, red = cells(first, beyond, x, squares, [got[name] for name in STARTS[4:]], lax.axis_size(GX_GZ))
     red = lax.all_to_all(red, GX_GZ, 0, 0)
     red = merge(red, lax.axis_size("gy"))
     red = lax.all_to_all(red, "gy", 0, 0)
-    hist, stats = final(red, first, beyond)
+    hist, stats = final(first, beyond, red)
     return mag, hist, stats
 
 

time: 79 us -> 76.7 us (0.971)
  blocking collectives: 13.1 us -> 29.6 us
  waiting for transfers between devices: 10.6 us -> 0.87 us
  starting transfers between devices: 38 us -> 30.6 us
  local copies, waits for them, and re-layouts: 0.97 us -> 0 us
    all_to_all x0 -> x1, blocking collectives: none -> 17.3 us  [on_device(): red = lax.all_to_all(red, 'gy', 0, 0)]
    all_to_all x1 -> x0, waiting for transfers between devices: 10.6 us -> none  [on_device(): red = lax.all_to_all(red, 'gy', 0, 0)]
    all_to_all x1 -> x0, starting transfers between devices: 8.65 us -> none  [on_device(): red = lax.all_to_all(red, 'gy', 0, 0)]
    ppermute x6, starting transfers between devices: 29.4 us -> 30.6 us  [swapped(): return lax.ppermute(part, axis, pairs + [(b, a) for a, b in pairs])]
    unnamed x1 -> x0, local copies, waits for them, and re-layouts: 0.97 us -> none
    ppermute x6, waiting for transfers between devices: 0.02 us -> 0.87 us  [swapped(): return lax.ppermute(part, axis, pairs + [(b, a) for a, b in pairs])]
  transfers between devices with their start and end apart: 7 -> 6, of which waited for: 1 -> 1; matrix products, arithmetic and copies ran while one was open for 1% -> 0% of each run, Pallas kernels for 5% -> 5%
where the time goes in v3:
time: 76.7 us; the launch traced here: 76.3 us
  starting transfers between devices  30.6 us (40%)
  blocking collectives  29.6 us (39%)
  Pallas kernels  13.2 us (17%)
  between operations  2.02 us (3%)
  waiting for transfers between devices  0.87 us (1%)
    ppermute x6, starting transfers between devices, swapped(): return lax.ppermute(part, axis, pairs + [(b, a) for a, b in pairs])  30.6 us
    all_to_all x1, blocking collectives, on_device(): red = lax.all_to_all(red, 'gy', 0, 0)  17.3 us
    all_to_all x1, blocking collectives, on_device(): red = lax.all_to_all(red, GX_GZ, 0, 0)  12.4 us
    pallas_call x1, Pallas kernels, cells(): pl.pallas_call(cells_kernel, in_specs=[SMEM, SMEM] + [VMEM] * 4, out_spec...  7.38 us
    pallas_call x1, Pallas kernels, xz_squares(): pl.pallas_call(xz_kernel, in_specs=[VMEM] * 8, out_specs=VMEM, out_shape=...  3.57 us
    pallas_call x1, Pallas kernels, pack(): pl.pallas_call(pack_kernel, in_specs=[pl.BlockSpec(memory_space=pl.ANY)],...  1.57 us
  transfers between devices with their start and end apart: 6, of which 1 were waited for; matrix products, arithmetic and copies ran while one was open for 0% of the time, Pallas kernels for 5%

profile of v3, /device:TPU:1, one launch (start us, length us, event | category | flops | bytes accessed | tf_op | source)
XLA Modules:
  0.0 76.3 jit_solution(13875225805562097252)
XLA Ops:
  0.6 1.6 %pack.1 = (f32[32,64,128]{2,1,0:T(8,128)S(1)}, f32[4,2048]{1,0:T(4,128)S(1)}, f32[4,2048]{1,0:T(4,128)S(1)}, f32[32,4,128]{2,1,0:T(4,128)S(1)}, f32[32,4,128]{2,...) custom-call(f32[32,64,128]{2,1,0:T(8,128)} %x_hbm.1), custom_call_target="tpu_custom_call" | custom-call | tf_op jit(solution)/shard_map/pack/pallas_call | solution.py:92
  2.2 3.9 %collective-permute-start.2 = (f32[4,64,128]{2,1,0:T(8,128)S(1)}, f32[4,64,128]{2,1,0:T(8,128)S(1)}, u32[]{:S(2)}, u32[]{:S(2)}) collective-permute-start(f32[4,64,128]{2,1,0:T(8,128)S(1)} %get-tuple-element.17), channel_id=1, source_target_pairs={{0,1},{2,3},{4,5},{6,7},{1,0},{3,2},{5,4},{7,6},{8,9},{10,11},{12,... | collective-permute-start | bytes 393224 | tf_op jit(solution)/shard_map/ppermute | solution.py:403
  6.2 4.7 %collective-permute-start.3 = (f32[4,64,128]{2,1,0:T(8,128)S(1)}, f32[4,64,128]{2,1,0:T(8,128)S(1)}, u32[]{:S(2)}, u32[]{:S(2)}) collective-permute-start(f32[4,64,128]{2,1,0:T(8,128)S(1)} %get-tuple-element.18), channel_id=1, source_target_pairs={{1,2},{3,4},{5,6},{7,0},{2,1},{4,3},{6,5},{0,7},{9,10},{11,12},{13... | collective-permute-start | bytes 393224 | tf_op jit(solution)/shard_map/ppermute | solution.py:403
  10.9 3.9 %collective-permute-start = (f32[4,2048]{1,0:T(4,128)S(1)}, f32[4,2048]{1,0:T(4,128)S(1)}, u32[]{:S(2)}, u32[]{:S(2)}) collective-permute-start(f32[4,2048]{1,0:T(4,128)S(1)} %get-tuple-element.15.xa_ref), channel_id=1, source_target_pairs={{0,128},{256,384},{128,0},{384,256},{1,129},{257,385},{129,1},{385... | collective-permute-start | bytes 98312 | tf_op jit(solution)/shard_map/ppermute | solution.py:403
  14.8 2.8 %collective-permute-start.4 = (f32[32,4,128]{2,1,0:T(4,128)S(1)}, f32[32,4,128]{2,1,0:T(4,128)S(1)}, u32[]{:S(2)}, u32[]{:S(2)}) collective-permute-start(f32[32,4,128]{2,1,0:T(4,128)S(1)} %get-tuple-element.19), channel_id=1, source_target_pairs={{0,8},{16,24},{32,40},{48,56},{64,72},{80,88},{96,104},{112,120},{... | collective-permute-start | bytes 196616 | tf_op jit(solution)/shard_map/ppermute | solution.py:403
  17.6 10.2 %collective-permute-start.5 = (f32[32,4,128]{2,1,0:T(4,128)S(1)}, f32[32,4,128]{2,1,0:T(4,128)S(1)}, u32[]{:S(2)}, u32[]{:S(2)}) collective-permute-start(f32[32,4,128]{2,1,0:T(4,128)S(1)} %get-tuple-element.20), channel_id=1, source_target_pairs={{8,16},{24,32},{40,48},{56,64},{72,80},{88,96},{104,112},{120,0},{... | collective-permute-start | bytes 196616 | tf_op jit(solution)/shard_map/ppermute | solution.py:403
  27.8 0.0 collective-permute-done.from_xa_ref
  27.8 5.0 %collective-permute-start.1 = (f32[4,2048]{1,0:T(4,128)S(1)}, f32[4,2048]{1,0:T(4,128)S(1)}, u32[]{:S(2)}, u32[]{:S(2)}) collective-permute-start(f32[4,2048]{1,0:T(4,128)S(1)} %get-tuple-element.16.xb_ref), channel_id=1, source_target_pairs={{128,256},{384,0},{256,128},{0,384},{129,257},{385,1},{257,129},{1... | collective-permute-start | bytes 98312 | tf_op jit(solution)/shard_map/ppermute | solution.py:403
  34.1 0.9 %collective-permute-done.1.from_xb_ref = f32[4,2048]{1,0:T(4,128)S(1)} collective-permute-done((f32[4,2048]{1,0:T(4,128)S(1)}, f32[4,2048]{1,0:T(4,128)S(1)}, u32[]{:S(2)}, u32[]{:S(2)}) %collective-permute-start.1) | collective-permute-done | bytes 32800 | tf_op jit(solution)/shard_map/ppermute | solution.py:403
  35.0 0.0 collective-permute-done.2.from_za_ref
  35.0 0.0 collective-permute-done.3.from_zb_ref
  35.0 3.6 %xz.1.square_ref = f32[32,64,128]{2,1,0:T(8,128)S(1)} custom-call(bf16[48,128]{1,0:T(8,128)(2,1)} %constant.2.clone.c_ref, f32[32,64,128]{2,1,0:T(8,128)S(1)} %get-tuple-element.14.x_ref, f32[4,2048]{1,0:T(4,128)S(1)} %get-tuple-element.15.xa_ref, f32[4,2048]{1,0:T(4,128)S(1)} %get-tuple-element.16.xb_ref, f32[4,2048]{1,0:T(4,128)S(1)} %collective-permute-done.from_xa_ref, ...), custom_call_target="tpu_custom_call" | custom-call | tf_op jit(solution)/shard_map/xz/pallas_call | solution.py:164
  38.6 0.0 collective-permute-done.4.from_ya_ref
  38.6 0.0 collective-permute-done.5.from_yb_ref
  38.6 7.4 %cells.1 = (f32[32,64,128]{2,1,0:T(8,128)S(1)}, f32[32,64,128]{2,1,0:T(8,128)}, f32[32,4,128]{2,1,0:T(4,128)S(1)}) custom-call(s32[1]{0:T(128)S(6)} %copy.9.first_ref, s32[1]{0:T(128)S(6)} %copy.10.beyond_ref, f32[32,64,128]{2,1,0:T(8,128)S(1)} %get-tuple-element.14.x_ref, f32[32,64,128]{2,1,0:T(8,128)S(1)} %xz.1.square_ref, ...), custom_call_target="tpu_custom_call", output_to_operand_aliasing={{0}: (3, {})} | custom-call | tf_op jit(solution)/shard_map/cells/pallas_call | solution.py:326
  46.0 12.4 %all_to_all.10.a_ref = f32[32,4,128]{2,1,0:T(4,128)S(1)} all-to-all(f32[32,4,128]{2,1,0:T(4,128)S(1)} %get-tuple-element.22), channel_id=1, replica_groups=mesh['gx_0'=2,'gx_1'=2,'gy'=16,'gz_0'=2,'gz_1'=4] {'gx_0','gx_1','gz_0',..., dimensions={0} | all-to-all | bytes 131072 | tf_op jit(solution)/shard_map/all_to_all | solution.py:417
  58.4 17.3 %all_to_all.11.a_ref = f32[16,4,128]{2,1,0:T(4,128)S(1)} all-to-all(f32[16,4,128]{2,1,0:T(4,128)S(1)} %merge.1), channel_id=1, replica_groups=mesh['gx_0'=2,'gx_1'=2,'gy'=16,'gz_0'=2,'gz_1'=4] {'gy'}, dimensions={0} | all-to-all | bytes 65536 | tf_op jit(solution)/shard_map/all_to_all | solution.py:419
  75.7 0.7 final.1
  (1 shorter events, 0.0 us)
Async XLA Ops:
  2.2 32.8 %collective-permute-start.2 = (f32[4,64,128]{2,1,0:T(8,128)S(1)}, f32[4,64,128]{2,1,0:T(8,128)S(1)}, u32[]{:S(2)}, u32[]{:S(2)}) collective-permute-start(f32[4,64,128]{2,1,0:T(8,128)S(1)} %get-tuple-element.17), channel_id=1, source_target_pairs={{0,1},{2,3},{4,5},{6,7},{1,0},{3,2},{5,4},{7,6},{8,9},{10,11},{12,... | collective-permute-start | bytes 393224 | tf_op jit(solution)/shard_map/ppermute | solution.py:403
  6.2 28.8 %collective-permute-start.3 = (f32[4,64,128]{2,1,0:T(8,128)S(1)}, f32[4,64,128]{2,1,0:T(8,128)S(1)}, u32[]{:S(2)}, u32[]{:S(2)}) collective-permute-start(f32[4,64,128]{2,1,0:T(8,128)S(1)} %get-tuple-element.18), channel_id=1, source_target_pairs={{1,2},{3,4},{5,6},{7,0},{2,1},{4,3},{6,5},{0,7},{9,10},{11,12},{13... | collective-permute-start | bytes 393224 | tf_op jit(solution)/shard_map/ppermute | solution.py:403
  10.9 16.9 %collective-permute-start = (f32[4,2048]{1,0:T(4,128)S(1)}, f32[4,2048]{1,0:T(4,128)S(1)}, u32[]{:S(2)}, u32[]{:S(2)}) collective-permute-start(f32[4,2048]{1,0:T(4,128)S(1)} %get-tuple-element.15.xa_ref), channel_id=1, source_target_pairs={{0,128},{256,384},{128,0},{384,256},{1,129},{257,385},{129,1},{385... | collective-permute-start | bytes 98312 | tf_op jit(solution)/shard_map/ppermute | solution.py:403
  14.8 23.7 %collective-permute-start.4 = (f32[32,4,128]{2,1,0:T(4,128)S(1)}, f32[32,4,128]{2,1,0:T(4,128)S(1)}, u32[]{:S(2)}, u32[]{:S(2)}) collective-permute-start(f32[32,4,128]{2,1,0:T(4,128)S(1)} %get-tuple-element.19), channel_id=1, source_target_pairs={{0,8},{16,24},{32,40},{48,56},{64,72},{80,88},{96,104},{112,120},{... | collective-permute-start | bytes 196616 | tf_op jit(solution)/shard_map/ppermute | solution.py:403
  17.6 21.0 %collective-permute-start.5 = (f32[32,4,128]{2,1,0:T(4,128)S(1)}, f32[32,4,128]{2,1,0:T(4,128)S(1)}, u32[]{:S(2)}, u32[]{:S(2)}) collective-permute-start(f32[32,4,128]{2,1,0:T(4,128)S(1)} %get-tuple-element.20), channel_id=1, source_target_pairs={{8,16},{24,32},{40,48},{56,64},{72,80},{88,96},{104,112},{120,0},{... | collective-permute-start | bytes 196616 | tf_op jit(solution)/shard_map/ppermute | solution.py:403
  27.8 7.1 %collective-permute-start.1 = (f32[4,2048]{1,0:T(4,128)S(1)}, f32[4,2048]{1,0:T(4,128)S(1)}, u32[]{:S(2)}, u32[]{:S(2)}) collective-permute-start(f32[4,2048]{1,0:T(4,128)S(1)} %get-tuple-element.16.xb_ref), channel_id=1, source_target_pairs={{128,256},{384,0},{256,128},{0,384},{129,257},{385,1},{257,129},{1... | collective-permute-start | bytes 98312 | tf_op jit(solution)/shard_map/ppermute | solution.py:403
